TPU v7x, 512 devices: a whole 4x8x8 slice. The times are simulated.
512 devices in a mesh: sub: 8 (over y), row: 8 (over x, core), col: 8 (over z).
Axes of the slice: x: 4, y: 8, z: 8, core: 2. Of those that a mesh axis runs over, the one named last changes fastest.
Arguments:
- visibility: bfloat16 [2, 64, 512, 4096], P(None, 'sub', 'row', 'col'), may hold values from -13 to 13
- sky_model: bfloat16 [2, 64, 512, 4096], P(None, 'sub', 'row', 'col'), may hold values from -4 to 4, as said below
- antenna_flags: int32 [8, 512], P('sub'), may hold values 0 or 1
- gains_init: float32 [2, 64, 512], P(None, 'sub'), may hold values from -0.5 to 1.5
Outputs:
- gains: float32 [2, 64, 512], P(None, 'sub')
Inputs may be any that keep to these rules, and one draw needn't show every extreme that they name: `sky_model`: model visibility parts lie between -4 and 4.
All inputs are finite; a program needn't handle non-finite values.
Results may differ from a plain program's by a relative error of at most 0.0003.
Values sent between devices are 32-bit elements.
No kernel may reach another device: no remote copies, remote signals or barrier semaphores. Data moves between devices by JAX's collectives and lax.ppermute only.
A program may use at most 64 MiB of HBM per device.

v0:
```python
import jax
import jax.numpy as jnp
from jax import lax
from jax.sharding import PartitionSpec as P

TIMES = 8
ITERS = 3


def copy_for_each(array, axis):
    devices = lax.axis_size(axis)
    return lax.all_to_all(
        jnp.broadcast_to(array[None], (devices, *array.shape)), axis, 0, 0, tiled=True
    )


def of_everyone(array, axis):
    return copy_for_each(array, axis).sum(axis=0)


def in_order(blocks, dim):
    shape = list(blocks.shape[1:])
    shape[dim] *= blocks.shape[0]
    return jnp.moveaxis(blocks, 0, dim).reshape(shape)


def collect(array, axis, dim):
    return in_order(copy_for_each(array, axis), dim)


def subband_total(values):
    return of_everyone(values, "sub")


def update_gains(summed, previous):
    denominator = summed[:, 2, :] + 1.0
    quotient = jnp.stack([summed[:, 0, :] / denominator, summed[:, 1, :] / denominator], axis=0)
    updated = 0.5 * (quotient + previous)
    chan_mean = jnp.sum(updated, axis=1) / updated.shape[1]
    overall = subband_total(chan_mean) / lax.axis_size("sub")
    return updated + 0.5 * (overall - chan_mean)[:, None, :]


def time_total(values, selector):
    return jnp.einsum(
        "crk,kq->crq",
        values,
        selector,
        precision=lax.Precision.HIGHEST,
        preferred_element_type=jnp.float32,
    )


def contract(matrix, vector):
    return jnp.einsum("cpq,cq->cp", matrix, vector, precision=lax.Precision.HIGHEST)


def body(visibility, sky_model, antenna_flags, gains_init):
    block_rows = visibility.shape[2]
    wide_cols = visibility.shape[3]
    block_cols = wide_cols // TIMES
    row_at = lax.axis_index("row") * block_rows
    col_at = lax.axis_index("col") * block_cols
    flag_value = antenna_flags[0].astype(jnp.float32)
    row_flag = lax.dynamic_slice_in_dim(flag_value, row_at, block_rows)
    col_flag = lax.dynamic_slice_in_dim(flag_value, col_at, block_cols)
    row_ids = row_at + lax.iota(jnp.int32, block_rows)
    col_ids = col_at + lax.iota(jnp.int32, block_cols)
    weight = (
        row_flag[:, None]
        * col_flag[None, :]
        * (row_ids[:, None] != col_ids[None, :]).astype(jnp.float32)
    )
    selector = (
        lax.iota(jnp.int32, wide_cols)[:, None] // TIMES == lax.iota(jnp.int32, block_cols)[None, :]
    ).astype(jnp.float32)
    vis_re = visibility[0].astype(jnp.float32)
    vis_im = visibility[1].astype(jnp.float32)
    mod_re = sky_model[0].astype(jnp.float32)
    mod_im = sky_model[1].astype(jnp.float32)
    cross_re = time_total(vis_re * mod_re + vis_im * mod_im, selector) * weight
    cross_im = time_total(vis_im * mod_re - vis_re * mod_im, selector) * weight
    power_sum = time_total(mod_re * mod_re + mod_im * mod_im, selector) * weight
    gain_values = gains_init
    for step_index in range(ITERS):
        col_gains = lax.dynamic_slice_in_dim(gain_values, col_at, block_cols, 2)
        gain_re = col_gains[0]
        gain_im = col_gains[1]
        num_re = contract(cross_re, gain_re) - contract(cross_im, gain_im)
        num_im = contract(cross_re, gain_im) + contract(cross_im, gain_re)
        denominator = contract(power_sum, gain_re * gain_re + gain_im * gain_im)
        partial_value = jnp.stack([num_re, num_im, denominator], axis=1)
        summed = of_everyone(partial_value, "col")
        previous = lax.dynamic_slice_in_dim(gain_values, row_at, block_rows, 2)
        gain_block = update_gains(summed, previous)
        gain_values = collect(gain_block, "row", 2)
    return gain_values


def solution(mesh):
    return jax.shard_map(
        body,
        mesh=mesh,
        in_specs=(
            P(None, "sub", "row", "col"),
            P(None, "sub", "row", "col"),
            P("sub", None),
            P(None, "sub", None),
        ),
        out_specs=P(None, "sub", None),
        check_vma=False,
    )
```

profile of v0, /device:TPU:1, one launch (start us, length us, event | category | flops | bytes accessed | tf_op | source)
XLA Modules:
  0.0 123.8 jit_solution(15700047814634009049)
XLA Ops:
  0.0 0.7 copy-done.1
  0.9 2.5 %convolution_multiply_fusion.1 = f32[8,64,64]{2,1,0:T(8,128)S(1)} fusion(bf16[2,8,64,512]{3,2,1,0:T(8,128)(2,1)} %param.4, bf16[2,8,64,512]{3,2,1,0:T(8,128)(2,1)} %param.5, f32[64,64]{1,0:T(8,128)S(1)} %multiply_select_fusion, s32[512]{0:T(512)S(1)} %add_select_fusion), kind=kOutput, calls=%fused_computation.7 | convolution fusion | flops 203227136 | bytes 2246656 | tf_op jit(solution)/shard_map/crk,kq->crq/dot_general | solution.py:45
  3.4 0.8 convolution_multiply_fusion.2
  4.3 0.5 fusion.49
  4.8 0.5 fusion.47
  5.4 0.5 fusion.48
  5.9 0.5 fusion.46
  6.4 0.8 convolution_multiply_fusion
  7.2 0.5 fusion.50
  7.8 0.1 reshape.309
  7.9 17.7 %all_to_all.45 = f32[8,1,1536]{2,1,0:T(1,128)S(1)} all-to-all(f32[8,1,1536]{2,1,0:T(1,128)S(1)} %reshape.309), channel_id=1, replica_groups=mesh['sub'=8,'row'=8,'col'=8] {'col'}, dimensions={0} | all-to-all | bytes 98304 | tf_op jit(solution)/shard_map/all_to_all | solution.py:12
  25.6 0.5 broadcast.242
  26.1 0.8 reduce
  27.0 0.1 fusion.43
  27.2 13.2 %all_to_all.46 = f32[8,1,128]{2,1,0:T(1,128)S(1)} all-to-all(f32[8,1,128]{2,1,0:T(1,128)S(1)} %reshape.311), channel_id=1, replica_groups=mesh['sub'=8,'row'=8,'col'=8] {'sub'}, dimensions={0} | all-to-all | bytes 8192 | tf_op jit(solution)/shard_map/all_to_all | solution.py:12
  40.3 0.7 reduce.1
  41.2 0.1 reshape.313
  41.3 12.3 %all_to_all.47 = f32[8,1,1024]{2,1,0:T(1,128)S(1)} all-to-all(f32[8,1,1024]{2,1,0:T(1,128)S(1)} %reshape.313), channel_id=1, replica_groups=mesh['sub'=8,'row'=8,'col'=8] {'row'}, dimensions={0} | all-to-all | bytes 65536 | tf_op jit(solution)/shard_map/all_to_all | solution.py:12
  53.7 0.7 reduce.2
  54.7 0.5 fusion.54
  55.2 0.5 fusion.51
  55.7 0.5 fusion.53
  56.2 0.5 fusion.52
  56.8 0.5 fusion.55
  57.3 0.1 reshape.315
  57.4 9.5 %all_to_all.48 = f32[8,1,1536]{2,1,0:T(1,128)S(1)} all-to-all(f32[8,1,1536]{2,1,0:T(1,128)S(1)} %reshape.315), channel_id=1, replica_groups=mesh['sub'=8,'row'=8,'col'=8] {'col'}, dimensions={0} | all-to-all | bytes 98304 | tf_op jit(solution)/shard_map/all_to_all | solution.py:12
  66.9 0.8 reduce.3
  67.8 0.1 fusion.42
  68.0 8.9 %all_to_all.49 = f32[8,1,128]{2,1,0:T(1,128)S(1)} all-to-all(f32[8,1,128]{2,1,0:T(1,128)S(1)} %reshape.317), channel_id=1, replica_groups=mesh['sub'=8,'row'=8,'col'=8] {'sub'}, dimensions={0} | all-to-all | bytes 8192 | tf_op jit(solution)/shard_map/all_to_all | solution.py:12
  76.9 0.7 reduce.4
  77.8 0.1 reshape.319
  77.9 10.1 %all_to_all.50 = f32[8,1,1024]{2,1,0:T(1,128)S(1)} all-to-all(f32[8,1,1024]{2,1,0:T(1,128)S(1)} %reshape.319), channel_id=1, replica_groups=mesh['sub'=8,'row'=8,'col'=8] {'row'}, dimensions={0} | all-to-all | bytes 65536 | tf_op jit(solution)/shard_map/all_to_all | solution.py:12
  88.0 0.7 reduce.5
  88.9 0.5 fusion.57
  89.5 0.5 fusion.58
  90.0 0.5 fusion.59
  90.5 0.5 fusion.56
  91.0 0.5 fusion.60
  91.6 0.1 reshape.321
  91.7 9.5 %all_to_all.51 = f32[8,1,1536]{2,1,0:T(1,128)S(1)} all-to-all(f32[8,1,1536]{2,1,0:T(1,128)S(1)} %reshape.321), channel_id=1, replica_groups=mesh['sub'=8,'row'=8,'col'=8] {'col'}, dimensions={0} | all-to-all | bytes 98304 | tf_op jit(solution)/shard_map/all_to_all | solution.py:12
  101.2 0.8 reduce.6
  102.1 0.1 fusion.41
  102.3 8.9 %all_to_all.52 = f32[8,1,128]{2,1,0:T(1,128)S(1)} all-to-all(f32[8,1,128]{2,1,0:T(1,128)S(1)} %reshape.323), channel_id=1, replica_groups=mesh['sub'=8,'row'=8,'col'=8] {'sub'}, dimensions={0} | all-to-all | bytes 8192 | tf_op jit(solution)/shard_map/all_to_all | solution.py:12
  111.2 0.7 reduce.7
  112.1 0.1 reshape.325
  112.2 10.1 %all_to_all.53 = f32[8,1,1024]{2,1,0:T(1,128)S(1)} all-to-all(f32[8,1,1024]{2,1,0:T(1,128)S(1)} %reshape.325), channel_id=1, replica_groups=mesh['sub'=8,'row'=8,'col'=8] {'row'}, dimensions={0} | all-to-all | bytes 65536 | tf_op jit(solution)/shard_map/all_to_all | solution.py:12
  122.2 0.7 reduce.8
  123.1 0.7 reshape.283
  (68 shorter events, 2.2 us)
Async XLA Ops:
  0.0 0.7 copy-start.1
  0.8 2.5 %copy-start.2 = (bf16[2,8,64,512]{3,2,1,0:T(8,128)(2,1)S(1)}, bf16[2,8,64,512]{3,2,1,0:T(8,128)(2,1)}, u32[]{:S(2)}) copy-start(bf16[2,8,64,512]{3,2,1,0:T(8,128)(2,1)} %param.4) | copy-start | bytes 3145732
  0.9 2.5 %copy-start.3 = (bf16[2,8,64,512]{3,2,1,0:T(8,128)(2,1)S(1)}, bf16[2,8,64,512]{3,2,1,0:T(8,128)(2,1)}, u32[]{:S(2)}) copy-start(bf16[2,8,64,512]{3,2,1,0:T(8,128)(2,1)} %param.5) | copy-start | bytes 3145732
  3.4 0.8 copy-start
where the time goes:
time: 124 us
  blocking collectives  100 us (81%)
  matrix products  11.9 us (10%)
  other arithmetic  7.49 us (6%)
  local copies, waits for them, and re-layouts  3.88 us (3%)
    all_to_all x9, blocking collectives, copy_for_each(): lax.all_to_all(jnp.broadcast_to(array[None], (devices, *array.shape)), ax...  100 us
    dot_general x15, matrix products, contract(): jnp.einsum('cpq,cq->cp', matrix, vector, precision=lax.Precision.HIGHEST)  7.86 us
    all_to_all x9, other arithmetic, copy_for_each(): lax.all_to_all(jnp.broadcast_to(array[None], (devices, *array.shape)), ax...  6.41 us
    dot_general x3, matrix products, time_total(): jnp.einsum('crk,kq->crq', values, selector, precision=lax.Precision.HIGHE...  4.08 us

commit v1 on v0

v1 whole, which is shorter than its diff:
```python
import jax
import jax.numpy as jnp
from jax import lax
from jax.experimental import pallas as pl
from jax.experimental.pallas import tpu as pltpu
from jax.sharding import PartitionSpec as P


TIMES = 8
PEERS = 8
HALF = 64
F32 = jnp.float32
VMEM = pl.BlockSpec(memory_space=pltpu.VMEM)


def low_lanes(rows):
    return lax.broadcasted_iota(jnp.int32, (rows, 128), 1) < HALF


def swap(value):
    return pltpu.roll(value, HALF, 1)


def own_half(slab, odd):
    return jnp.where(odd, swap(slab), slab)


def spread(gains):
    turned = gains.T
    low = low_lanes(HALF)
    columns = []
    for row in range(8):
        first = jnp.broadcast_to(turned[:HALF, row : row + 1], (HALF, 128))
        second = jnp.broadcast_to(turned[HALF:, row : row + 1], (HALF, 128))
        columns.append(jnp.where(low, first, second))
    return columns[:4], columns[4:]


def products(cross_re, cross_im, power, gain_re, gain_im):
    over = lambda value: jnp.sum(value, axis=0, keepdims=True)
    return (
        over(cross_re * gain_re - cross_im * gain_im),
        over(cross_re * gain_im + cross_im * gain_re),
        over(power * (gain_re * gain_re + gain_im * gain_im)),
    )


def contract(tile, gains, sums):
    gain_re, gain_im = spread(gains)
    for j in range(4):
        rows = products(tile[0, j], tile[1, j], tile[2, j], gain_re[j], gain_im[j])
        for part in range(3):
            sums[part * 4 + j : part * 4 + j + 1, :] = rows[part]


def first_kernel(vis, sky, flags, init, tile, message, weight, gain, selector, sums):
    j = pl.program_id(0)
    row = lax.axis_index("row")
    col = lax.axis_index("col")

    @pl.when(j == 0)
    def _():
        low = low_lanes(4)

        def block(ref, index, lead):
            start = pl.multiple_of(lax.shift_right_logical(index, 1) * 128, 128)
            return own_half(ref[lead + (slice(None), pl.ds(start, 128))], lax.rem(index, 2) == 1)

        packed = []
        for part in range(2):
            mine = block(init, col, (part,))
            packed.append(jnp.where(low, mine[:4], swap(mine)[4:]))
        gain_re, gain_im = spread(jnp.concatenate(packed, axis=0))
        for k in range(4):
            gain[0, k] = gain_re[k]
            gain[1, k] = gain_im[k]
        row_flag = block(flags, row, ()).astype(F32)
        row_flag = jnp.where(low_lanes(1), row_flag, swap(row_flag))
        col_flag = jnp.broadcast_to(block(flags, col, ()).astype(F32), (8, 128)).T[:HALF, 0:1]
        col_ids = col * HALF + lax.broadcasted_iota(jnp.int32, (HALF, 128), 0)
        row_ids = row * HALF + (lax.broadcasted_iota(jnp.int32, (HALF, 128), 1) & (HALF - 1))
        weight[...] = jnp.where(col_ids != row_ids, col_flag * row_flag, 0.0)
        wide = lax.broadcasted_iota(jnp.int32, (HALF, HALF * TIMES), 1)
        narrow = lax.broadcasted_iota(jnp.int32, (HALF, HALF * TIMES), 0)
        selector[...] = jnp.where(lax.shift_right_logical(wide, 3) == narrow, 1.0, 0.0).astype(jnp.bfloat16)

    def wide_part(ref, part):
        return ref[part, :, 0].reshape(128, HALF * TIMES).astype(F32)

    vis_re, vis_im = wide_part(vis, 0), wide_part(vis, 1)
    mod_re, mod_im = wide_part(sky, 0), wide_part(sky, 1)
    chosen = selector[...]

    def time_total(value):
        high = value.astype(jnp.bfloat16)
        rest = (value - high.astype(F32)).astype(jnp.bfloat16)
        dims = (((1,), (1,)), ((), ()))
        total = lax.dot_general(chosen, high, dims, preferred_element_type=F32)
        return total + lax.dot_general(chosen, rest, dims, preferred_element_type=F32)

    scale = weight[...]
    cross_re = time_total(vis_re * mod_re + vis_im * mod_im) * scale
    cross_im = time_total(vis_im * mod_re - vis_re * mod_im) * scale
    power = time_total(mod_re * mod_re + mod_im * mod_im) * scale
    tile[0, 0] = cross_re
    tile[1, 0] = cross_im
    tile[2, 0] = power
    rows = products(cross_re, cross_im, power, gain[0, j], gain[1, j])
    for part in range(3):
        sums[pl.ds(part * 4 + j, 1), :] = rows[part]

    @pl.when(j == 3)
    def _():
        for peer in range(PEERS):
            message[peer] = sums[...]


def update(summed, previous, mean, rest):
    denominator = summed[8:12] + 1.0
    updated = 0.5 * (jnp.concatenate([summed[0:4] / denominator, summed[4:8] / denominator], axis=0) + previous)
    means = []
    kept = []
    for part in range(2):
        values = updated[part * 4 : part * 4 + 4]
        total = jnp.sum(values, axis=0, keepdims=True)
        total = (total + swap(total)) / 8.0
        means.append(total)
        kept.append(values - 0.5 * total)
    mean[...] = jnp.broadcast_to(jnp.where(low_lanes(1), means[0], means[1]), (PEERS, 128))
    rest[...] = jnp.concatenate(kept, axis=0)


def first_update_kernel(received, init, mean, rest):
    row = lax.axis_index("row")
    start = pl.multiple_of(lax.shift_right_logical(row, 1) * 128, 128)
    low = low_lanes(4)
    packed = []
    for part in range(2):
        mine = own_half(init[part, :, pl.ds(start, 128)], lax.rem(row, 2) == 1)
        packed.append(jnp.where(low, mine[:4], swap(mine)[4:]))
    update(jnp.sum(received[...], axis=0), jnp.concatenate(packed, axis=0), mean, rest)


def update_kernel(owner, received, mean, rest):
    previous = received[lax.axis_index(owner), 12:20]
    update(jnp.sum(received[:, 0:12], axis=0), previous, mean, rest)


def add_overall(means, rest):
    overall = jnp.sum(means[...], axis=0, keepdims=True) / 16.0
    other = swap(overall)
    low = low_lanes(1)
    return jnp.concatenate(
        [rest[0:4] + jnp.where(low, overall, other), rest[4:8] + jnp.where(low, other, overall)], axis=0
    )


def contract_kernel(means, rest, tile, message, sums):
    gains = add_overall(means, rest)
    contract(tile, gains, sums)
    sums[12:20, :] = gains
    sums[20:24, :] = jnp.zeros((4, 128), F32)
    for peer in range(PEERS):
        message[peer] = sums[...]


def share_kernel(means, rest, message):
    gains = add_overall(means, rest)
    for peer in range(PEERS):
        message[peer] = gains


def collect_kernel(received, out):
    low = low_lanes(4)
    for part in range(2):
        for pair in range(4):
            even = received[2 * pair, part * 4 : part * 4 + 4]
            odd = received[2 * pair + 1, part * 4 : part * 4 + 4]
            out[part, 0:4, pair * 128 : pair * 128 + 128] = jnp.where(low, even, swap(odd))
            out[part, 4:8, pair * 128 : pair * 128 + 128] = jnp.where(low, swap(even), odd)


def shaped(*shape):
    return jax.ShapeDtypeStruct(shape, F32)


def call(kernel, outs, *args, scratch=()):
    return pl.pallas_call(
        kernel,
        out_shape=outs,
        in_specs=[VMEM] * len(args),
        out_specs=jax.tree.map(lambda _: VMEM, outs),
        scratch_shapes=scratch,
        compiler_params=pltpu.CompilerParams(vmem_limit_bytes=4 << 20),
        name=kernel.__name__,
    )(*args)


def exchange(message, axis):
    return lax.all_to_all(message, axis, 0, 0, tiled=True)


def body(visibility, sky_model, antenna_flags, gains_init):
    wide = (2, 2, 4, HALF, HALF * TIMES)
    whole = lambda shape: pl.BlockSpec(shape, lambda j: (0,) * len(shape))
    data = pl.BlockSpec((2, 2, 1, HALF, HALF * TIMES), lambda j: (0, 0, j, 0, 0))
    tile, message = pl.pallas_call(
        first_kernel,
        grid=(4,),
        out_shape=(shaped(3, 4, HALF, 128), shaped(PEERS, 12, 128)),
        in_specs=[data, data, whole((1, 512)), whole((2, 8, 512))],
        out_specs=(pl.BlockSpec((3, 1, HALF, 128), lambda j: (0, j, 0, 0)), whole((PEERS, 12, 128))),
        scratch_shapes=[
            pltpu.VMEM((HALF, 128), F32),
            pltpu.VMEM((2, 4, HALF, 128), F32),
            pltpu.VMEM((HALF, HALF * TIMES), jnp.bfloat16),
            pltpu.VMEM((12, 128), F32),
        ],
        compiler_params=pltpu.CompilerParams(vmem_limit_bytes=12 << 20),
        name="first_kernel",
    )(visibility.reshape(wide), sky_model.reshape(wide), antenna_flags, gains_init)
    outs = (shaped(PEERS, 128), shaped(8, 128))
    sums = [pltpu.VMEM((24, 128), F32)]

    received = exchange(message, "col")
    mean, rest = call(first_update_kernel, outs, received, gains_init)
    tile, mean = lax.optimization_barrier((tile, mean))
    turned = lax.ppermute(
        tile, ("row", "col"), [(r * 8 + c, c * 8 + r) for r in range(8) for c in range(8)]
    )
    means = exchange(mean, "sub")
    message = call(contract_kernel, shaped(PEERS, 24, 128), means, rest, turned, scratch=sums)
    received = exchange(message, "row")

    def after_row(received, mean, rest):
        update_kernel("col", received, mean, rest)

    def after_col(received, mean, rest):
        update_kernel("row", received, mean, rest)

    mean, rest = call(after_row, outs, received)
    means = exchange(mean, "sub")
    message = call(contract_kernel, shaped(PEERS, 24, 128), means, rest, tile, scratch=sums)
    received = exchange(message, "col")
    mean, rest = call(after_col, outs, received)
    means = exchange(mean, "sub")
    message = call(share_kernel, shaped(PEERS, 8, 128), means, rest)
    received = exchange(message, "row")
    return call(collect_kernel, shaped(2, 8, 512), received)


def solution(mesh):
    return jax.shard_map(
        body,
        mesh=mesh,
        in_specs=(
            P(None, "sub", "row", "col"),
            P(None, "sub", "row", "col"),
            P("sub", None),
            P(None, "sub", None),
        ),
        out_specs=P(None, "sub", None),
        check_vma=False,
    )
```

time: 124 us -> 113 us (0.911)
  matrix products: 11.9 us -> 0 us
  other arithmetic: 7.49 us -> 0 us
  Pallas kernels: 0 us -> 4.84 us
  starting transfers between devices: 0 us -> 4.17 us
    dot_general x18 -> x0, matrix products: 11.9 us -> none  [the longest x15 7.86 us: contract(): jnp.einsum('cpq,cq->cp', matrix, vector, precision=lax.Precision.HIGHEST)]
    all_to_all x9 -> x0, other arithmetic: 6.41 us -> none  [copy_for_each(): lax.all_to_all(jnp.broadcast_to(array[None], (devices, *array.shape)), ax...]
    pallas_call x0 -> x8, Pallas kernels: none -> 4.84 us  [the longest x1 2.72 us: body(): pl.pallas_call(first_kernel, grid=(4,), out_shape=(shaped(3, 4, HALF, 128...]
    ppermute x0 -> x1, starting transfers between devices: none -> 4.17 us  [body(): lax.ppermute(tile, ('row', 'col'), [(r * 8 + c, c * 8 + r) for r in range...]
    unnamed x29 -> x8, local copies, waits for them, and re-layouts: 2.33 us -> 3.89 us
    all_to_all x9 -> x7, blocking collectives: 100 us -> 99.2 us  [exchange(): return lax.all_to_all(message, axis, 0, 0, tiled=True)]
  transfers between devices with their start and end apart: 0 -> 1, of which waited for: 0 -> 0; matrix products, arithmetic and copies ran while one was open for 0% -> 0% of each run, Pallas kernels for 0% -> 0%
where the time goes in v1:
time: 113 us; the launch traced here: 112 us
  blocking collectives  99.2 us (88%)
  Pallas kernels  4.84 us (4%)
  starting transfers between devices  4.17 us (4%)
  local copies, waits for them, and re-layouts  3.89 us (3%)
    all_to_all x7, blocking collectives, exchange(): return lax.all_to_all(message, axis, 0, 0, tiled=True)  99.2 us
    ppermute x1, starting transfers between devices, body(): lax.ppermute(tile, ('row', 'col'), [(r * 8 + c, c * 8 + r) for r in range...  4.17 us
    unnamed x8, local copies, waits for them, and re-layouts  3.89 us
    pallas_call x1, Pallas kernels, body(): pl.pallas_call(first_kernel, grid=(4,), out_shape=(shaped(3, 4, HALF, 128...  2.72 us
  transfers between devices with their start and end apart: 1, of which 0 were waited for; matrix products, arithmetic and copies ran while one was open for 0% of the time, Pallas kernels for 0%

profile of v1, /device:TPU:1, one launch (start us, length us, event | category | flops | bytes accessed | tf_op | source)
XLA Modules:
  0.0 112.1 jit_solution(6658726535370808397)
XLA Ops:
  0.0 0.0 copy-start.3
  0.0 0.7 copy-done.3
  0.7 0.0 copy-start
  0.7 1.2 %copy-done = bf16[2,8,64,512]{3,2,1,0:T(8,128)(2,1)S(1)} copy-done((bf16[2,8,64,512]{3,2,1,0:T(8,128)(2,1)S(1)}, bf16[2,8,64,512]{3,2,1,0:T(8,128)(2,1)}, u32[]{:S(2)}) %copy-start) | copy-done | bytes 1048600
  1.9 0.0 copy-start.1
  1.9 1.2 %copy-done.1 = bf16[2,8,64,512]{3,2,1,0:T(8,128)(2,1)S(1)} copy-done((bf16[2,8,64,512]{3,2,1,0:T(8,128)(2,1)S(1)}, bf16[2,8,64,512]{3,2,1,0:T(8,128)(2,1)}, u32[]{:S(2)}) %copy-start.1) | copy-done | bytes 1048600
  3.1 0.0 copy-start.2
  3.1 0.8 copy-done.2
  3.9 2.7 %first_kernel.1 = (f32[3,4,64,128]{3,2,1,0:T(8,128)S(1)}, f32[8,12,128]{2,1,0:T(8,128)S(1)}) custom-call(bf16[2,2,4,64,512]{4,3,2,1,0:T(8,128)(2,1)S(1)} %bitcast.14, bf16[2,2,4,64,512]{4,3,2,1,0:T(8,128)(2,1)S(1)} %bitcast.15, s32[1,512]{1,0:T(1,128)S(1)} %copy-done.3, f32[2,8,512]{2,1,0:T(8,128)S(1)} %copy-done.2), custom_call_target="tpu_custom_call" | custom-call | tf_op jit(solution)/shard_map/first_kernel/pallas_call | solution.py:207
  6.6 17.9 %all_to_all.53.received = f32[8,12,128]{2,1,0:T(8,128)S(1)} all-to-all(f32[8,12,128]{2,1,0:T(8,128)S(1)} %get-tuple-element.16), channel_id=1, replica_groups=mesh['sub'=8,'row'=8,'col'=8] {'col'}, dimensions={0} | all-to-all | bytes 98304 | tf_op jit(solution)/shard_map/all_to_all | solution.py:200
  24.5 0.2 first_update_kernel.1
  24.7 4.2 %collective-permute-start = (f32[3,4,64,128]{3,2,1,0:T(8,128)S(1)}, f32[3,4,64,128]{3,2,1,0:T(8,128)S(1)}, u32[]{:S(2)}, u32[]{:S(2)}) collective-permute-start(f32[3,4,64,128]{3,2,1,0:T(8,128)S(1)} %get-tuple-element.20.tile), channel_id=1, source_target_pairs={{0,0},{1,8},{2,16},{3,24},{4,32},{5,40},{6,48},{7,56},{8,1},{9,9},... | collective-permute-start | bytes 1179656 | tf_op jit(solution)/shard_map/ppermute | solution.py:228
  28.9 13.2 %all_to_all.54 = f32[8,1,128]{2,1,0:T(1,128)S(1)} all-to-all(f32[8,1,128]{2,1,0:T(1,128)S(1)} %bitcast.19), channel_id=1, replica_groups=mesh['sub'=8,'row'=8,'col'=8] {'sub'}, dimensions={0} | all-to-all | bytes 8192 | tf_op jit(solution)/shard_map/all_to_all | solution.py:200
  42.1 0.0 collective-permute-done.tile
  42.1 0.5 contract_kernel.2
  42.6 24.5 %all_to_all.55.received = f32[8,24,128]{2,1,0:T(8,128)S(1)} all-to-all(f32[8,24,128]{2,1,0:T(8,128)S(1)} %contract_kernel.2), channel_id=1, replica_groups=mesh['sub'=8,'row'=8,'col'=8] {'row'}, dimensions={0} | all-to-all | bytes 196608 | tf_op jit(solution)/shard_map/all_to_all | solution.py:200
  67.0 0.1 after_row.1
  67.1 13.2 %all_to_all.56 = f32[8,1,128]{2,1,0:T(1,128)S(1)} all-to-all(f32[8,1,128]{2,1,0:T(1,128)S(1)} %bitcast.20), channel_id=1, replica_groups=mesh['sub'=8,'row'=8,'col'=8] {'sub'}, dimensions={0} | all-to-all | bytes 8192 | tf_op jit(solution)/shard_map/all_to_all | solution.py:200
  80.3 0.5 contract_kernel.3
  80.7 10.0 %all_to_all.57.received = f32[8,24,128]{2,1,0:T(8,128)S(1)} all-to-all(f32[8,24,128]{2,1,0:T(8,128)S(1)} %contract_kernel.3), channel_id=1, replica_groups=mesh['sub'=8,'row'=8,'col'=8] {'col'}, dimensions={0} | all-to-all | bytes 196608 | tf_op jit(solution)/shard_map/all_to_all | solution.py:200
  90.7 0.1 after_col.1
  90.8 8.9 %all_to_all.58 = f32[8,1,128]{2,1,0:T(1,128)S(1)} all-to-all(f32[8,1,128]{2,1,0:T(1,128)S(1)} %bitcast.21), channel_id=1, replica_groups=mesh['sub'=8,'row'=8,'col'=8] {'sub'}, dimensions={0} | all-to-all | bytes 8192 | tf_op jit(solution)/shard_map/all_to_all | solution.py:200
  99.7 0.1 share_kernel.1
  99.8 11.6 %all_to_all.59.received = f32[8,8,128]{2,1,0:T(8,128)S(1)} all-to-all(f32[8,8,128]{2,1,0:T(8,128)S(1)} %share_kernel.1), channel_id=1, replica_groups=mesh['sub'=8,'row'=8,'col'=8] {'row'}, dimensions={0} | all-to-all | bytes 65536 | tf_op jit(solution)/shard_map/all_to_all | solution.py:200
  111.4 0.7 collect_kernel.1
Async XLA Ops:
  0.0 0.7 copy-start.3
  0.7 1.2 %copy-start = (bf16[2,8,64,512]{3,2,1,0:T(8,128)(2,1)S(1)}, bf16[2,8,64,512]{3,2,1,0:T(8,128)(2,1)}, u32[]{:S(2)}) copy-start(bf16[2,8,64,512]{3,2,1,0:T(8,128)(2,1)} %param.4) | copy-start | bytes 3145732
  1.9 1.2 %copy-start.1 = (bf16[2,8,64,512]{3,2,1,0:T(8,128)(2,1)S(1)}, bf16[2,8,64,512]{3,2,1,0:T(8,128)(2,1)}, u32[]{:S(2)}) copy-start(bf16[2,8,64,512]{3,2,1,0:T(8,128)(2,1)} %param.5) | copy-start | bytes 3145732
  3.1 0.8 copy-start.2
  24.7 17.4 %collective-permute-start = (f32[3,4,64,128]{3,2,1,0:T(8,128)S(1)}, f32[3,4,64,128]{3,2,1,0:T(8,128)S(1)}, u32[]{:S(2)}, u32[]{:S(2)}) collective-permute-start(f32[3,4,64,128]{3,2,1,0:T(8,128)S(1)} %get-tuple-element.20.tile), channel_id=1, source_target_pairs={{0,0},{1,8},{2,16},{3,24},{4,32},{5,40},{6,48},{7,56},{8,1},{9,9},... | collective-permute-start | bytes 1179656 | tf_op jit(solution)/shard_map/ppermute | solution.py:228

commit v2 on v1

--- a/solution.py
+++ b/solution.py
@@ -10,6 +10,7 @@
 PEERS = 8
 HALF = 64
 F32 = jnp.float32
+FIRST_LIMIT = 16 << 20
 VMEM = pl.BlockSpec(memory_space=pltpu.VMEM)
 
 
@@ -53,43 +54,45 @@
             sums[part * 4 + j : part * 4 + j + 1, :] = rows[part]
 
 
-def first_kernel(vis, sky, flags, init, tile, message, weight, gain, selector, sums):
-    j = pl.program_id(0)
+def first_kernel(vis_hbm, sky_hbm, flags_hbm, init_hbm, tile, message, vis, sky, flags, init, sums, small_sems, wide_sems):
     row = lax.axis_index("row")
     col = lax.axis_index("col")
-
-    @pl.when(j == 0)
-    def _():
-        low = low_lanes(4)
-
-        def block(ref, index, lead):
-            start = pl.multiple_of(lax.shift_right_logical(index, 1) * 128, 128)
-            return own_half(ref[lead + (slice(None), pl.ds(start, 128))], lax.rem(index, 2) == 1)
-
-        packed = []
-        for part in range(2):
-            mine = block(init, col, (part,))
-            packed.append(jnp.where(low, mine[:4], swap(mine)[4:]))
-        gain_re, gain_im = spread(jnp.concatenate(packed, axis=0))
-        for k in range(4):
-            gain[0, k] = gain_re[k]
-            gain[1, k] = gain_im[k]
-        row_flag = block(flags, row, ()).astype(F32)
-        row_flag = jnp.where(low_lanes(1), row_flag, swap(row_flag))
-        col_flag = jnp.broadcast_to(block(flags, col, ()).astype(F32), (8, 128)).T[:HALF, 0:1]
-        col_ids = col * HALF + lax.broadcasted_iota(jnp.int32, (HALF, 128), 0)
-        row_ids = row * HALF + (lax.broadcasted_iota(jnp.int32, (HALF, 128), 1) & (HALF - 1))
-        weight[...] = jnp.where(col_ids != row_ids, col_flag * row_flag, 0.0)
-        wide = lax.broadcasted_iota(jnp.int32, (HALF, HALF * TIMES), 1)
-        narrow = lax.broadcasted_iota(jnp.int32, (HALF, HALF * TIMES), 0)
-        selector[...] = jnp.where(lax.shift_right_logical(wide, 3) == narrow, 1.0, 0.0).astype(jnp.bfloat16)
-
-    def wide_part(ref, part):
-        return ref[part, :, 0].reshape(128, HALF * TIMES).astype(F32)
-
-    vis_re, vis_im = wide_part(vis, 0), wide_part(vis, 1)
-    mod_re, mod_im = wide_part(sky, 0), wide_part(sky, 1)
-    chosen = selector[...]
+    small = [
+        pltpu.make_async_copy(flags_hbm, flags, small_sems.at[0]),
+        pltpu.make_async_copy(init_hbm, init, small_sems.at[1]),
+    ]
+    wide = [
+        [
+            pltpu.make_async_copy(source.at[:, :, j], target.at[j], wide_sems.at[which, j])
+            for which, (source, target) in enumerate(((vis_hbm, vis), (sky_hbm, sky)))
+        ]
+        for j in range(4)
+    ]
+    for copy in small + sum(wide, []):
+        copy.start()
+
+    long = lax.broadcasted_iota(jnp.int32, (HALF, HALF * TIMES), 1)
+    short = lax.broadcasted_iota(jnp.int32, (HALF, HALF * TIMES), 0)
+    chosen = jnp.where(lax.shift_right_logical(long, 3) == short, 1.0, 0.0).astype(jnp.bfloat16)
+    for copy in small:
+        copy.wait()
+    low = low_lanes(4)
+
+    def block(ref, index, lead):
+        start = pl.multiple_of(lax.shift_right_logical(index, 1) * 128, 128)
+        return own_half(ref[lead + (slice(None), pl.ds(start, 128))], lax.rem(index, 2) == 1)
+
+    packed = []
+    for part in range(2):
+        mine = block(init, col, (part,))
+        packed.append(jnp.where(low, mine[:4], swap(mine)[4:]))
+    gain_re, gain_im = spread(jnp.concatenate(packed, axis=0))
+    row_flag = block(flags, row, ()).astype(F32)
+    row_flag = jnp.where(low_lanes(1), row_flag, swap(row_flag))
+    col_flag = jnp.broadcast_to(block(flags, col, ()).astype(F32), (8, 128)).T[:HALF, 0:1]
+    col_ids = col * HALF + lax.broadcasted_iota(jnp.int32, (HALF, 128), 0)
+    row_ids = row * HALF + (lax.broadcasted_iota(jnp.int32, (HALF, 128), 1) & (HALF - 1))
+    scale = jnp.where(col_ids != row_ids, col_flag * row_flag, 0.0)
 
     def time_total(value):
         high = value.astype(jnp.bfloat16)
@@ -98,21 +101,26 @@
         total = lax.dot_general(chosen, high, dims, preferred_element_type=F32)
         return total + lax.dot_general(chosen, rest, dims, preferred_element_type=F32)
 
-    scale = weight[...]
-    cross_re = time_total(vis_re * mod_re + vis_im * mod_im) * scale
-    cross_im = time_total(vis_im * mod_re - vis_re * mod_im) * scale
-    power = time_total(mod_re * mod_re + mod_im * mod_im) * scale
-    tile[0, 0] = cross_re
-    tile[1, 0] = cross_im
-    tile[2, 0] = power
-    rows = products(cross_re, cross_im, power, gain[0, j], gain[1, j])
-    for part in range(3):
-        sums[pl.ds(part * 4 + j, 1), :] = rows[part]
-
-    @pl.when(j == 3)
-    def _():
-        for peer in range(PEERS):
-            message[peer] = sums[...]
+    for j in range(4):
+        for copy in wide[j]:
+            copy.wait()
+
+        def wide_part(ref, part):
+            return ref[j, part].reshape(128, HALF * TIMES).astype(F32)
+
+        vis_re, vis_im = wide_part(vis, 0), wide_part(vis, 1)
+        mod_re, mod_im = wide_part(sky, 0), wide_part(sky, 1)
+        cross_re = time_total(vis_re * mod_re + vis_im * mod_im) * scale
+        cross_im = time_total(vis_im * mod_re - vis_re * mod_im) * scale
+        power = time_total(mod_re * mod_re + mod_im * mod_im) * scale
+        tile[0, j] = cross_re
+        tile[1, j] = cross_im
+        tile[2, j] = power
+        rows = products(cross_re, cross_im, power, gain_re[j], gain_im[j])
+        for part in range(3):
+            sums[part * 4 + j : part * 4 + j + 1, :] = rows[part]
+    for peer in range(PEERS):
+        message[peer] = sums[...]
 
 
 def update(summed, previous, mean, rest):
@@ -202,29 +210,29 @@
 
 def body(visibility, sky_model, antenna_flags, gains_init):
     wide = (2, 2, 4, HALF, HALF * TIMES)
-    whole = lambda shape: pl.BlockSpec(shape, lambda j: (0,) * len(shape))
-    data = pl.BlockSpec((2, 2, 1, HALF, HALF * TIMES), lambda j: (0, 0, j, 0, 0))
+    stay = pl.BlockSpec(memory_space=pl.ANY)
     tile, message = pl.pallas_call(
         first_kernel,
-        grid=(4,),
         out_shape=(shaped(3, 4, HALF, 128), shaped(PEERS, 12, 128)),
-        in_specs=[data, data, whole((1, 512)), whole((2, 8, 512))],
-        out_specs=(pl.BlockSpec((3, 1, HALF, 128), lambda j: (0, j, 0, 0)), whole((PEERS, 12, 128))),
+        in_specs=[stay] * 4,
+        out_specs=(VMEM, VMEM),
         scratch_shapes=[
-            pltpu.VMEM((HALF, 128), F32),
-            pltpu.VMEM((2, 4, HALF, 128), F32),
-            pltpu.VMEM((HALF, HALF * TIMES), jnp.bfloat16),
+            pltpu.VMEM((4, 2, 2, HALF, HALF * TIMES), jnp.bfloat16),
+            pltpu.VMEM((4, 2, 2, HALF, HALF * TIMES), jnp.bfloat16),
+            pltpu.VMEM((1, 512), jnp.int32),
+            pltpu.VMEM((2, 8, 512), F32),
             pltpu.VMEM((12, 128), F32),
+            pltpu.SemaphoreType.DMA((2,)),
+            pltpu.SemaphoreType.DMA((2, 4)),
         ],
-        compiler_params=pltpu.CompilerParams(vmem_limit_bytes=12 << 20),
+        compiler_params=pltpu.CompilerParams(vmem_limit_bytes=FIRST_LIMIT),
         name="first_kernel",
-    )(visibility.reshape(wide), sky_model.reshape(wide), antenna_flags, gains_init)
+    )(*[pltpu.with_memory_space_constraint(x, pltpu.HBM) for x in (visibility.reshape(wide), sky_model.reshape(wide), antenna_flags, gains_init)])
     outs = (shaped(PEERS, 128), shaped(8, 128))
     sums = [pltpu.VMEM((24, 128), F32)]
 
     received = exchange(message, "col")
     mean, rest = call(first_update_kernel, outs, received, gains_init)
-    tile, mean = lax.optimization_barrier((tile, mean))
     turned = lax.ppermute(
         tile, ("row", "col"), [(r * 8 + c, c * 8 + r) for r in range(8) for c in range(8)]
     )

time: 113 us -> 113 us (level)
  local copies, waits for them, and re-layouts: 3.89 us -> 0.01 us
  blocking collectives: 99.2 us -> 101 us
  Pallas kernels: 4.84 us -> 6.22 us
  starting transfers between devices: 4.17 us -> 5.38 us
    unnamed x8 -> x2, local copies, waits for them, and re-layouts: 3.89 us -> 0.01 us
    all_to_all x7, blocking collectives: 99.2 us -> 101 us  [exchange(): return lax.all_to_all(message, axis, 0, 0, tiled=True)]
    pallas_call x1, Pallas kernels: 2.72 us -> 4.1 us  [body(): pl.pallas_call(first_kernel, out_shape=(shaped(3, 4, HALF, 128), shaped(P...]
    ppermute x1, starting transfers between devices: 4.17 us -> 5.38 us  [body(): lax.ppermute(tile, ('row', 'col'), [(r * 8 + c, c * 8 + r) for r in range...]
where the time goes in v2:
time: 113 us
  blocking collectives  101 us (89%)
  Pallas kernels  6.22 us (6%)
  starting transfers between devices  5.38 us (5%)
    all_to_all x7, blocking collectives, exchange(): return lax.all_to_all(message, axis, 0, 0, tiled=True)  101 us
    ppermute x1, starting transfers between devices, body(): lax.ppermute(tile, ('row', 'col'), [(r * 8 + c, c * 8 + r) for r in range...  5.38 us
    pallas_call x1, Pallas kernels, body(): pl.pallas_call(first_kernel, out_shape=(shaped(3, 4, HALF, 128), shaped(P...  4.1 us
  transfers between devices with their start and end apart: 1, of which 0 were waited for; matrix products, arithmetic and copies ran while one was open for 0% of the time, Pallas kernels for 0%

profile of v2, /device:TPU:1, one launch (start us, length us, event | category | flops | bytes accessed | tf_op | source)
XLA Modules:
  0.0 112.5 jit_solution(3875735002901957623)
XLA Ops:
  0.0 4.1 %first_kernel.1 = (f32[3,4,64,128]{3,2,1,0:T(8,128)S(1)}, f32[8,12,128]{2,1,0:T(8,128)S(1)}) custom-call(bf16[2,2,4,64,512]{4,3,2,1,0:T(8,128)(2,1)} %bitcast.20, bf16[2,2,4,64,512]{4,3,2,1,0:T(8,128)(2,1)} %bitcast.21, s32[1,512]{1,0:T(1,128)} %flags_hbm.1, f32[2,8,512]{2,1,0:T(8,128)} %init.1), custom_call_target="tpu_custom_call" | custom-call | tf_op jit(solution)/shard_map/first_kernel/pallas_call | solution.py:214
  4.1 5.4 %collective-permute-start = (f32[3,4,64,128]{3,2,1,0:T(8,128)S(1)}, f32[3,4,64,128]{3,2,1,0:T(8,128)S(1)}, u32[]{:S(2)}, u32[]{:S(2)}) collective-permute-start(f32[3,4,64,128]{3,2,1,0:T(8,128)S(1)} %get-tuple-element.16.tile), channel_id=1, source_target_pairs={{0,0},{1,8},{2,16},{3,24},{4,32},{5,40},{6,48},{7,56},{8,1},{9,9},... | collective-permute-start | bytes 1179656 | tf_op jit(solution)/shard_map/ppermute | solution.py:236
  9.5 0.0 copy-start
  9.5 33.9 %all_to_all.53.received = f32[8,12,128]{2,1,0:T(8,128)S(1)} all-to-all(f32[8,12,128]{2,1,0:T(8,128)S(1)} %get-tuple-element.13), channel_id=1, replica_groups=mesh['sub'=8,'row'=8,'col'=8] {'col'}, dimensions={0} | all-to-all | bytes 98304 | tf_op jit(solution)/shard_map/all_to_all | solution.py:208
  43.4 0.0 copy-done
  43.4 0.2 first_update_kernel.1
  43.7 13.2 %all_to_all.54 = f32[8,1,128]{2,1,0:T(1,128)S(1)} all-to-all(f32[8,1,128]{2,1,0:T(1,128)S(1)} %bitcast.17), channel_id=1, replica_groups=mesh['sub'=8,'row'=8,'col'=8] {'sub'}, dimensions={0} | all-to-all | bytes 8192 | tf_op jit(solution)/shard_map/all_to_all | solution.py:208
  56.8 0.0 collective-permute-done.tile
  56.8 0.5 contract_kernel.2
  57.3 12.0 %all_to_all.55.received = f32[8,24,128]{2,1,0:T(8,128)S(1)} all-to-all(f32[8,24,128]{2,1,0:T(8,128)S(1)} %contract_kernel.2), channel_id=1, replica_groups=mesh['sub'=8,'row'=8,'col'=8] {'row'}, dimensions={0} | all-to-all | bytes 196608 | tf_op jit(solution)/shard_map/all_to_all | solution.py:208
  69.3 0.1 after_row.1
  69.4 8.9 %all_to_all.56 = f32[8,1,128]{2,1,0:T(1,128)S(1)} all-to-all(f32[8,1,128]{2,1,0:T(1,128)S(1)} %bitcast.18), channel_id=1, replica_groups=mesh['sub'=8,'row'=8,'col'=8] {'sub'}, dimensions={0} | all-to-all | bytes 8192 | tf_op jit(solution)/shard_map/all_to_all | solution.py:208
  78.3 0.4 contract_kernel.3
  78.8 12.4 %all_to_all.57.received = f32[8,24,128]{2,1,0:T(8,128)S(1)} all-to-all(f32[8,24,128]{2,1,0:T(8,128)S(1)} %contract_kernel.3), channel_id=1, replica_groups=mesh['sub'=8,'row'=8,'col'=8] {'col'}, dimensions={0} | all-to-all | bytes 196608 | tf_op jit(solution)/shard_map/all_to_all | solution.py:208
  91.2 0.1 after_col.1
  91.3 8.9 %all_to_all.58 = f32[8,1,128]{2,1,0:T(1,128)S(1)} all-to-all(f32[8,1,128]{2,1,0:T(1,128)S(1)} %bitcast.19), channel_id=1, replica_groups=mesh['sub'=8,'row'=8,'col'=8] {'sub'}, dimensions={0} | all-to-all | bytes 8192 | tf_op jit(solution)/shard_map/all_to_all | solution.py:208
  100.2 0.1 share_kernel.1
  100.3 11.5 %all_to_all.59.received = f32[8,8,128]{2,1,0:T(8,128)S(1)} all-to-all(f32[8,8,128]{2,1,0:T(8,128)S(1)} %share_kernel.1), channel_id=1, replica_groups=mesh['sub'=8,'row'=8,'col'=8] {'row'}, dimensions={0} | all-to-all | bytes 65536 | tf_op jit(solution)/shard_map/all_to_all | solution.py:208
  111.8 0.7 collect_kernel.1
Async XLA Ops:
  4.1 52.7 %collective-permute-start = (f32[3,4,64,128]{3,2,1,0:T(8,128)S(1)}, f32[3,4,64,128]{3,2,1,0:T(8,128)S(1)}, u32[]{:S(2)}, u32[]{:S(2)}) collective-permute-start(f32[3,4,64,128]{3,2,1,0:T(8,128)S(1)} %get-tuple-element.16.tile), channel_id=1, source_target_pairs={{0,0},{1,8},{2,16},{3,24},{4,32},{5,40},{6,48},{7,56},{8,1},{9,9},... | collective-permute-start | bytes 1179656 | tf_op jit(solution)/shard_map/ppermute | solution.py:236
  9.5 33.9 %copy-start = (f32[2,8,512]{2,1,0:T(8,128)S(1)}, f32[2,8,512]{2,1,0:T(8,128)}, u32[]{:S(2)}) copy-start(f32[2,8,512]{2,1,0:T(8,128)} %init.1) | copy-start | bytes 98308

commit v3 on v2

v3 whole, which is shorter than its diff:
```python
import functools

import jax
import jax.numpy as jnp
from jax import lax
from jax.experimental import pallas as pl
from jax.experimental.pallas import tpu as pltpu
from jax.sharding import PartitionSpec as P


TIMES = 8
PEERS = 8
HALF = 64
F32 = jnp.float32
FIRST_LIMIT = 16 << 20
TILE_ROWS = 96
VMEM = pl.BlockSpec(memory_space=pltpu.VMEM)


def low_lanes(rows):
    return lax.broadcasted_iota(jnp.int32, (rows, 128), 1) < HALF


def swap(value):
    return pltpu.roll(value, HALF, 1)


def own_half(slab, odd):
    return jnp.where(odd, swap(slab), slab)


def spread(gains):
    turned = gains.T
    low = low_lanes(HALF)
    columns = []
    for row in range(8):
        first = jnp.broadcast_to(turned[:HALF, row : row + 1], (HALF, 128))
        second = jnp.broadcast_to(turned[HALF:, row : row + 1], (HALF, 128))
        columns.append(jnp.where(low, first, second))
    return columns[:4], columns[4:]


def products(cross_re, cross_im, power, gain_re, gain_im):
    over = lambda value: jnp.sum(value, axis=0, keepdims=True)
    return (
        over(cross_re * gain_re - cross_im * gain_im),
        over(cross_re * gain_im + cross_im * gain_re),
        over(power * (gain_re * gain_re + gain_im * gain_im)),
    )


def lanes_of(rows):
    return lax.broadcasted_iota(jnp.int32, (rows, 128), 1)


def slide(value, step):
    line = lax.broadcasted_iota(jnp.int32, (8, 128), 0)
    for bit in (1, 2, 4):
        value = jnp.where((line & bit) != 0, pltpu.roll(value, (step * bit) % 128, 1), value)
    return value


def pack(wide, which):
    lane = lanes_of(8)
    near = pltpu.roll(wide, (128 - 8 * which) % 128, 1)
    far = pltpu.roll(wide, (200 - 8 * which) % 128, 1)
    value = jnp.where(lane < 8, near, jnp.where(lane < 16, far, 0.0))
    return jnp.sum(slide(value, 16), axis=0, keepdims=True)


def pack_all(wide):
    return jnp.concatenate([pack(wide, which) for which in range(8)], axis=0)


def unpack(packed):
    group = lax.shift_right_logical(lanes_of(8), 3)
    wide = jnp.zeros((8, 128), F32)
    for which in range(8):
        line = jnp.broadcast_to(packed[which : which + 1], (8, 128))
        line = slide(line, -16)
        near = pltpu.roll(line, 8 * which, 1)
        far = pltpu.roll(line, (8 * which + 56) % 128, 1)
        wide = jnp.where(group == which, near, jnp.where(group == which + 8, far, wide))
    return wide


def channel_mean(packed):
    lane = lanes_of(8) & (HALF - 1)
    total = packed
    for step in (8, 16, 32):
        total = total + jnp.where(lane >= step, pltpu.roll(total, step, 1), pltpu.roll(total, step + HALF, 1))
    return total / 8.0


def smoothed(updated, sub):
    overall = jnp.sum(updated[...], axis=0) / 8.0
    own = updated[sub]
    return own + 0.5 * channel_mean(overall - own)


def spread_packed(gains):
    turned = gains.T
    low = low_lanes(8)
    columns = []
    for row in range(8):
        pieces = []
        for which in range(8):
            first = jnp.broadcast_to(turned[row * 16 : row * 16 + 8, which : which + 1], (8, 128))
            second = jnp.broadcast_to(turned[row * 16 + 8 : row * 16 + 16, which : which + 1], (8, 128))
            pieces.append(jnp.where(low, first, second))
        columns.append(pieces)
    return columns[:4], columns[4:]


def contract(tile, gains, sums):
    gain_re, gain_im = spread_packed(gains)
    for j in range(4):
        totals = [jnp.zeros((8, 128), F32)] * 3
        for which in range(8):
            cross_re, cross_im, power = [
                tile[which, (part * 4 + j) * 8 : (part * 4 + j) * 8 + 8] for part in range(3)
            ]
            re, im = gain_re[j][which], gain_im[j][which]
            totals[0] += cross_re * re - cross_im * im
            totals[1] += cross_re * im + cross_im * re
            totals[2] += power * (re * re + im * im)
        for part in range(3):
            sums[part * 4 + j : part * 4 + j + 1, :] = jnp.sum(totals[part], axis=0, keepdims=True)


def first_kernel(vis_hbm, sky_hbm, flags_hbm, init_hbm, message, previous, vis, sky, flags, init, sums, small_sems, wide_sems):
    row = lax.axis_index("row")
    col = lax.axis_index("col")
    small = [
        pltpu.make_async_copy(flags_hbm, flags, small_sems.at[0]),
        pltpu.make_async_copy(init_hbm, init, small_sems.at[1]),
    ]
    wide = [
        [
            pltpu.make_async_copy(source.at[:, :, j], target.at[j], wide_sems.at[which, j])
            for which, (source, target) in enumerate(((vis_hbm, vis), (sky_hbm, sky)))
        ]
        for j in range(4)
    ]
    for copy in small + sum(wide, []):
        copy.start()

    long = lax.broadcasted_iota(jnp.int32, (HALF, HALF * TIMES), 1)
    short = lax.broadcasted_iota(jnp.int32, (HALF, HALF * TIMES), 0)
    chosen = jnp.where(lax.shift_right_logical(long, 3) == short, 1.0, 0.0).astype(jnp.bfloat16)
    for copy in small:
        copy.wait()
    low = low_lanes(4)

    def block(ref, index, lead):
        start = pl.multiple_of(lax.shift_right_logical(index, 1) * 128, 128)
        return own_half(ref[lead + (slice(None), pl.ds(start, 128))], lax.rem(index, 2) == 1)

    def wide_gains(index):
        parts = []
        for part in range(2):
            mine = block(init, index, (part,))
            parts.append(jnp.where(low, mine[:4], swap(mine)[4:]))
        return jnp.concatenate(parts, axis=0)

    previous[...] = pack(wide_gains(row), col)
    gain_re, gain_im = spread(wide_gains(col))
    row_flag = block(flags, row, ()).astype(F32)
    row_flag = jnp.where(low_lanes(1), row_flag, swap(row_flag))
    col_flag = jnp.broadcast_to(block(flags, col, ()).astype(F32), (8, 128)).T[:HALF, 0:1]
    col_ids = col * HALF + lax.broadcasted_iota(jnp.int32, (HALF, 128), 0)
    row_ids = row * HALF + (lax.broadcasted_iota(jnp.int32, (HALF, 128), 1) & (HALF - 1))
    scale = jnp.where(col_ids != row_ids, col_flag * row_flag, 0.0)

    def time_total(value):
        high = value.astype(jnp.bfloat16)
        rest = (value - high.astype(F32)).astype(jnp.bfloat16)
        dims = (((1,), (1,)), ((), ()))
        total = lax.dot_general(chosen, high, dims, preferred_element_type=F32)
        return total + lax.dot_general(chosen, rest, dims, preferred_element_type=F32)

    for j in range(4):
        for copy in wide[j]:
            copy.wait()

        def wide_part(ref, part):
            return ref[j, part].reshape(128, HALF * TIMES).astype(F32)

        vis_re, vis_im = wide_part(vis, 0), wide_part(vis, 1)
        mod_re, mod_im = wide_part(sky, 0), wide_part(sky, 1)
        cross_re = time_total(vis_re * mod_re + vis_im * mod_im) * scale
        cross_im = time_total(vis_im * mod_re - vis_re * mod_im) * scale
        power = time_total(mod_re * mod_re + mod_im * mod_im) * scale
        for part, value in enumerate((cross_re, cross_im, power)):
            for peer in range(PEERS):
                at = (part * 4 + j) * 8
                message[peer, at : at + 8] = value[peer * 8 : peer * 8 + 8]
        rows = products(cross_re, cross_im, power, gain_re[j], gain_im[j])
        for part in range(3):
            sums[part * 4 + j : part * 4 + j + 1, :] = rows[part]
    sums[12:16, :] = jnp.zeros((4, 128), F32)
    for peer in range(PEERS):
        message[peer, TILE_ROWS:] = sums[...]


def updated_gains(numerator, denominator, previous):
    return 0.5 * (numerator / (denominator + 1.0) + previous)


def twice(rows):
    return jnp.concatenate([rows, rows], axis=0)


def update_kernel(start, received, previous, message):
    summed = jnp.sum(received[:, start : start + 16], axis=0)
    col = lax.axis_index("col")
    updated = updated_gains(pack(summed[0:8], col), pack(twice(summed[8:12]), col), previous[...])
    message[...] = jnp.broadcast_to(updated, message.shape)


def iterate_kernel(updated, tile, message, previous, gains_of, sums):
    gains = smoothed(updated, lax.axis_index("sub"))
    gains_of[...] = gains
    previous[...] = gains_of[pl.ds(lax.axis_index("row"), 1), :]
    contract(tile, gains, sums)
    sums[12:13, :] = previous[...]
    sums[13:16, :] = jnp.zeros((3, 128), F32)
    for peer in range(PEERS):
        message[peer] = sums[...]


def last_update_kernel(received, message):
    summed = jnp.sum(received[:, 0:12], axis=0)
    previous = jnp.concatenate([received[peer, 12:13] for peer in range(PEERS)], axis=0)
    updated = updated_gains(pack_all(summed[0:8]), pack_all(twice(summed[8:12])), previous)
    for peer in range(PEERS):
        message[peer] = updated


def share_kernel(updated, message):
    gains = unpack(smoothed(updated, lax.axis_index("sub")))
    for peer in range(PEERS):
        message[peer] = gains


def collect_kernel(received, out):
    low = low_lanes(4)
    for part in range(2):
        for pair in range(4):
            even = received[2 * pair, part * 4 : part * 4 + 4]
            odd = received[2 * pair + 1, part * 4 : part * 4 + 4]
            out[part, 0:4, pair * 128 : pair * 128 + 128] = jnp.where(low, even, swap(odd))
            out[part, 4:8, pair * 128 : pair * 128 + 128] = jnp.where(low, swap(even), odd)


def shaped(*shape):
    return jax.ShapeDtypeStruct(shape, F32)


def call(name, kernel, outs, *args, scratch=()):
    return pl.pallas_call(
        kernel,
        out_shape=outs,
        in_specs=[VMEM] * len(args),
        out_specs=jax.tree.map(lambda _: VMEM, outs),
        scratch_shapes=scratch,
        compiler_params=pltpu.CompilerParams(vmem_limit_bytes=4 << 20),
        name=name,
    )(*args)


def exchange(message, axis):
    return lax.all_to_all(message, axis, 0, 0, tiled=True)


def body(visibility, sky_model, antenna_flags, gains_init):
    wide = (2, 2, 4, HALF, HALF * TIMES)
    stay = pl.BlockSpec(memory_space=pl.ANY)
    message, previous = pl.pallas_call(
        first_kernel,
        out_shape=(shaped(PEERS, TILE_ROWS + 16, 128), shaped(1, 128)),
        in_specs=[stay] * 4,
        out_specs=(VMEM, VMEM),
        scratch_shapes=[
            pltpu.VMEM((4, 2, 2, HALF, HALF * TIMES), jnp.bfloat16),
            pltpu.VMEM((4, 2, 2, HALF, HALF * TIMES), jnp.bfloat16),
            pltpu.VMEM((1, 512), jnp.int32),
            pltpu.VMEM((2, 8, 512), F32),
            pltpu.VMEM((16, 128), F32),
            pltpu.SemaphoreType.DMA((2,)),
            pltpu.SemaphoreType.DMA((2, 4)),
        ],
        compiler_params=pltpu.CompilerParams(vmem_limit_bytes=FIRST_LIMIT),
        name="first_kernel",
    )(
        *[
            pltpu.with_memory_space_constraint(value, pltpu.HBM)
            for value in (visibility.reshape(wide), sky_model.reshape(wide), antenna_flags, gains_init)
        ]
    )
    tile = received = exchange(message, "col")
    scratch = [pltpu.VMEM((8, 128), F32), pltpu.VMEM((16, 128), F32)]
    for start in (TILE_ROWS, 0):
        kernel = functools.partial(update_kernel, start)
        message = call("update_kernel", kernel, shaped(PEERS * PEERS, 128), received, previous)
        updated = exchange(message, ("sub", "row")).reshape(PEERS, PEERS, 128)
        outs = (shaped(PEERS, 16, 128), shaped(1, 128))
        message, previous = call("iterate_kernel", iterate_kernel, outs, updated, tile, scratch=scratch)
        received = exchange(message, "col")
    message = call("last_update_kernel", last_update_kernel, shaped(PEERS, 8, 128), received)
    updated = exchange(message, "sub")
    message = call("share_kernel", share_kernel, shaped(PEERS, 8, 128), updated)
    received = exchange(message, "row")
    return call("collect_kernel", collect_kernel, shaped(2, 8, 512), received)


def solution(mesh):
    return jax.shard_map(
        body,
        mesh=mesh,
        in_specs=(
            P(None, "sub", "row", "col"),
            P(None, "sub", "row", "col"),
            P("sub", None),
            P(None, "sub", None),
        ),
        out_specs=P(None, "sub", None),
        check_vma=False,
    )
```

time: 113 us -> 108 us (0.956)
  starting transfers between devices: 5.38 us -> 0 us
  Pallas kernels: 6.22 us -> 7.7 us
    ppermute x1 -> x0, starting transfers between devices: 5.38 us -> none  [body(): lax.ppermute(tile, ('row', 'col'), [(r * 8 + c, c * 8 + r) for r in range...]
    pallas_call x7, Pallas kernels: 2.12 us -> 3.49 us  [call(): pl.pallas_call(kernel, out_shape=outs, in_specs=[VMEM] * len(args), out_s...]
  transfers between devices with their start and end apart: 1 -> 0, of which waited for: 0 -> 0; matrix products, arithmetic and copies ran while one was open for 0% -> 0% of each run, Pallas kernels for 0% -> 0%
where the time goes in v3:
time: 108 us
  blocking collectives  100 us (93%)
  Pallas kernels  7.7 us (7%)
    all_to_all x7, blocking collectives, exchange(): return lax.all_to_all(message, axis, 0, 0, tiled=True)  100 us
    pallas_call x1, Pallas kernels, body(): pl.pallas_call(first_kernel, out_shape=(shaped(PEERS, TILE_ROWS + 16, 128...  4.21 us
    pallas_call x7, Pallas kernels, call(): pl.pallas_call(kernel, out_shape=outs, in_specs=[VMEM] * len(args), out_s...  3.49 us

profile of v3, /device:TPU:1, one launch (start us, length us, event | category | flops | bytes accessed | tf_op | source)
XLA Modules:
  0.0 107.8 jit_solution(265361438842963118)
XLA Ops:
  0.0 4.2 %first_kernel.1 = (f32[8,112,128]{2,1,0:T(8,128)S(1)}, f32[1,128]{1,0:T(1,128)S(1)}) custom-call(bf16[2,2,4,64,512]{4,3,2,1,0:T(8,128)(2,1)} %bitcast.14, bf16[2,2,4,64,512]{4,3,2,1,0:T(8,128)(2,1)} %bitcast.15, s32[1,512]{1,0:T(1,128)} %flags_hbm.1, f32[2,8,512]{2,1,0:T(8,128)} %init_hbm.1), custom_call_target="tpu_custom_call" | custom-call | tf_op jit(solution)/shard_map/first_kernel/pallas_call | solution.py:279
  4.2 25.4 %all_to_all.43.received.tile = f32[8,112,128]{2,1,0:T(8,128)S(1)} all-to-all(f32[8,112,128]{2,1,0:T(8,128)S(1)} %get-tuple-element.10), channel_id=1, replica_groups=mesh['sub'=8,'row'=8,'col'=8] {'col'}, dimensions={0} | all-to-all | bytes 917504 | tf_op jit(solution)/shard_map/all_to_all | solution.py:273
  29.6 0.3 update_kernel.2
  29.9 21.6 %all_to_all.44 = f32[64,1,128]{2,1,0:T(1,128)S(1)} all-to-all(f32[64,1,128]{2,1,0:T(1,128)S(1)} %bitcast.11), channel_id=1, replica_groups=mesh['sub'=8,'row'=8,'col'=8] {'sub','row'}, dimensions={0} | all-to-all | bytes 65536 | tf_op jit(solution)/shard_map/all_to_all | solution.py:273
  51.5 0.6 iterate_kernel.2
  52.2 9.6 %all_to_all.45.received = f32[8,16,128]{2,1,0:T(8,128)S(1)} all-to-all(f32[8,16,128]{2,1,0:T(8,128)S(1)} %get-tuple-element.12), channel_id=1, replica_groups=mesh['sub'=8,'row'=8,'col'=8] {'col'}, dimensions={0} | all-to-all | bytes 131072 | tf_op jit(solution)/shard_map/all_to_all | solution.py:273
  61.8 0.3 update_kernel.3
  62.1 14.6 %all_to_all.46 = f32[64,1,128]{2,1,0:T(1,128)S(1)} all-to-all(f32[64,1,128]{2,1,0:T(1,128)S(1)} %bitcast.10), channel_id=1, replica_groups=mesh['sub'=8,'row'=8,'col'=8] {'sub','row'}, dimensions={0} | all-to-all | bytes 65536 | tf_op jit(solution)/shard_map/all_to_all | solution.py:273
  76.6 0.7 iterate_kernel.3
  77.4 9.6 %all_to_all.47.received = f32[8,16,128]{2,1,0:T(8,128)S(1)} all-to-all(f32[8,16,128]{2,1,0:T(8,128)S(1)} %get-tuple-element.14), channel_id=1, replica_groups=mesh['sub'=8,'row'=8,'col'=8] {'col'}, dimensions={0} | all-to-all | bytes 131072 | tf_op jit(solution)/shard_map/all_to_all | solution.py:273
  87.0 0.3 last_update_kernel.1
  87.3 9.2 %all_to_all.48.updated = f32[8,8,128]{2,1,0:T(8,128)S(1)} all-to-all(f32[8,8,128]{2,1,0:T(8,128)S(1)} %last_update_kernel.1), channel_id=1, replica_groups=mesh['sub'=8,'row'=8,'col'=8] {'sub'}, dimensions={0} | all-to-all | bytes 65536 | tf_op jit(solution)/shard_map/all_to_all | solution.py:273
  96.5 0.5 share_kernel.1
  97.1 10.1 %all_to_all.49.received = f32[8,8,128]{2,1,0:T(8,128)S(1)} all-to-all(f32[8,8,128]{2,1,0:T(8,128)S(1)} %share_kernel.1), channel_id=1, replica_groups=mesh['sub'=8,'row'=8,'col'=8] {'row'}, dimensions={0} | all-to-all | bytes 65536 | tf_op jit(solution)/shard_map/all_to_all | solution.py:273
  107.1 0.7 collect_kernel.1

commit v4 on v3

v4 whole, which is shorter than its diff:
```python
import functools

import jax
import jax.numpy as jnp
from jax import lax
from jax.experimental import pallas as pl
from jax.experimental.pallas import tpu as pltpu
from jax.sharding import PartitionSpec as P


TIMES = 8
PEERS = 8
HALF = 64
F32 = jnp.float32
FIRST_LIMIT = 16 << 20
TILE_ROWS = 96
VMEM = pl.BlockSpec(memory_space=pltpu.VMEM)


def low_lanes(rows):
    return lax.broadcasted_iota(jnp.int32, (rows, 128), 1) < HALF


def swap(value):
    return pltpu.roll(value, HALF, 1)


def own_half(slab, odd):
    return jnp.where(odd, swap(slab), slab)


def spread_row(turned, row):
    first = jnp.broadcast_to(turned[:HALF, row : row + 1], (HALF, 128))
    second = jnp.broadcast_to(turned[HALF:, row : row + 1], (HALF, 128))
    return jnp.where(low_lanes(HALF), first, second)


def products(cross_re, cross_im, power, gain_re, gain_im):
    over = lambda value: jnp.sum(value, axis=0, keepdims=True)
    return (
        over(cross_re * gain_re - cross_im * gain_im),
        over(cross_re * gain_im + cross_im * gain_re),
        over(power * (gain_re * gain_re + gain_im * gain_im)),
    )


def lanes_of(rows):
    return lax.broadcasted_iota(jnp.int32, (rows, 128), 1)


def slide(value, step):
    line = lax.broadcasted_iota(jnp.int32, (8, 128), 0)
    out = value
    for row in range(1, 8):
        out = jnp.where(line == row, pltpu.roll(value, (step * row) % 128, 1), out)
    return out


def pack_all(wide):
    lane = lanes_of(8)
    own = lax.shift_right_logical(lane, 4) == lax.broadcasted_iota(jnp.int32, (8, 128), 0)
    near = own & ((lane & 8) == 0)
    far = own & ((lane & 8) != 0)
    moved = slide(wide, 16)
    rows = []
    for which in range(8):
        first = pltpu.roll(moved, (128 - 8 * which) % 128, 1)
        second = pltpu.roll(moved, (200 - 8 * which) % 128, 1)
        value = jnp.where(near, first, jnp.where(far, second, 0.0))
        rows.append(jnp.sum(value, axis=0, keepdims=True))
    return rows


def unpack(packed, which):
    group = lax.shift_right_logical(lanes_of(8), 3)
    moved = slide(jnp.broadcast_to(packed, (8, 128)), 112)
    first = pltpu.roll(moved, 8 * which, 1)
    second = pltpu.roll(moved, (8 * which + 56) % 128, 1)
    return jnp.where(group == which, first, jnp.where(group == which + 8, second, 0.0))


def channel_mean(packed):
    lane = lanes_of(8) & (HALF - 1)
    total = packed
    for step in range(8, HALF, 8):
        total = total + jnp.where(lane >= step, pltpu.roll(packed, step, 1), pltpu.roll(packed, step + HALF, 1))
    return total / 8.0


def smoothed(updated, sub):
    overall = jnp.sum(updated[...], axis=0) / 8.0
    own = updated[sub]
    return own + 0.5 * channel_mean(overall - own)


def spread_packed(gains):
    turned = gains.T
    low = low_lanes(8)
    columns = []
    for row in range(8):
        pieces = []
        for which in range(8):
            first = jnp.broadcast_to(turned[row * 16 : row * 16 + 8, which : which + 1], (8, 128))
            second = jnp.broadcast_to(turned[row * 16 + 8 : row * 16 + 16, which : which + 1], (8, 128))
            pieces.append(jnp.where(low, first, second))
        columns.append(pieces)
    return columns[:4], columns[4:]


def contract(tile, gains, sums):
    gain_re, gain_im = spread_packed(gains)
    for j in range(4):
        totals = [jnp.zeros((8, 128), F32)] * 3
        for which in range(8):
            cross_re, cross_im, power = [
                tile[which, (part * 4 + j) * 8 : (part * 4 + j) * 8 + 8] for part in range(3)
            ]
            re, im = gain_re[j][which], gain_im[j][which]
            totals[0] += cross_re * re - cross_im * im
            totals[1] += cross_re * im + cross_im * re
            totals[2] += power * (re * re + im * im)
        for part in range(3):
            sums[part * 4 + j : part * 4 + j + 1, :] = jnp.sum(totals[part], axis=0, keepdims=True)


def twice(rows):
    return jnp.concatenate([rows, rows], axis=0)


def share_sums(summed, message, start):
    numerators = pack_all(summed[0:8])
    denominators = pack_all(twice(summed[8:12]))
    for peer in range(PEERS):
        rows = [numerators[peer], denominators[peer], jnp.zeros((6, 128), F32)]
        message[peer, start : start + 8] = jnp.concatenate(rows, axis=0)


def first_kernel(vis_hbm, sky_hbm, flags_hbm, init_hbm, message, previous, vis, sky, flags, init, parts, gain, sums, small_sems, wide_sems):
    row = lax.axis_index("row")
    col = lax.axis_index("col")
    small = [
        pltpu.make_async_copy(flags_hbm, flags, small_sems.at[0]),
        pltpu.make_async_copy(init_hbm, init, small_sems.at[1]),
    ]
    wide = [
        [
            pltpu.make_async_copy(source.at[:, :, j], target.at[j], wide_sems.at[which, j])
            for which, (source, target) in enumerate(((vis_hbm, vis), (sky_hbm, sky)))
        ]
        for j in range(4)
    ]
    for copy in small + sum(wide, []):
        copy.start()

    long = lax.broadcasted_iota(jnp.int32, (HALF, HALF * TIMES), 1)
    short = lax.broadcasted_iota(jnp.int32, (HALF, HALF * TIMES), 0)
    chosen = jnp.where(lax.shift_right_logical(long, 3) == short, 1.0, 0.0).astype(jnp.bfloat16)
    for copy in small + wide[0]:
        copy.wait()
    low = low_lanes(4)

    def block(ref, index, lead):
        start = pl.multiple_of(lax.shift_right_logical(index, 1) * 128, 128)
        return own_half(ref[lead + (slice(None), pl.ds(start, 128))], lax.rem(index, 2) == 1)

    def wide_gains(index):
        parts = []
        for part in range(2):
            mine = block(init, index, (part,))
            parts.append(jnp.where(low, mine[:4], swap(mine)[4:]))
        return jnp.concatenate(parts, axis=0)

    mine = pack_all(wide_gains(row))
    chosen_row = mine[0]
    for which in range(1, 8):
        chosen_row = jnp.where(col == which, mine[which], chosen_row)
    previous[...] = chosen_row
    row_flag = block(flags, row, ()).astype(F32)
    row_flag = jnp.where(low_lanes(1), row_flag, swap(row_flag))
    col_flag = jnp.broadcast_to(block(flags, col, ()).astype(F32), (8, 128)).T[:HALF, 0:1]
    col_ids = col * HALF + lax.broadcasted_iota(jnp.int32, (HALF, 128), 0)
    row_ids = row * HALF + (lax.broadcasted_iota(jnp.int32, (HALF, 128), 1) & (HALF - 1))
    scale = jnp.where(col_ids != row_ids, col_flag * row_flag, 0.0)

    dims = (((1,), (1,)), ((), ()))

    def split(j, piece):
        half, at, lanes = piece // 8, piece // 2 % 4 * 16, pl.ds(piece % 2 * 256, 256)
        rows = pl.ds(half * HALF + at, 16)
        vis_re, vis_im = [vis[j, part, half, pl.ds(at, 16), lanes].astype(F32) for part in range(2)]
        mod_re, mod_im = [sky[j, part, half, pl.ds(at, 16), lanes].astype(F32) for part in range(2)]
        values = (
            vis_re * mod_re + vis_im * mod_im,
            vis_im * mod_re - vis_re * mod_im,
            mod_re * mod_re + mod_im * mod_im,
        )
        for which, value in enumerate(values):
            high = value.astype(jnp.bfloat16)
            parts[j % 2, 2 * which, rows, lanes] = high
            parts[j % 2, 2 * which + 1, rows, lanes] = (value - high.astype(F32)).astype(jnp.bfloat16)

    def time_total(j, which):
        high = lax.dot_general(chosen, parts[j % 2, 2 * which], dims, preferred_element_type=F32)
        rest = lax.dot_general(chosen, parts[j % 2, 2 * which + 1], dims, preferred_element_type=F32)
        value = (high + rest) * scale
        for peer in range(PEERS):
            at = (which * 4 + j) * 8
            message[peer, at : at + 8] = value[peer * 8 : peer * 8 + 8]
        return value

    turned = wide_gains(col).T
    for step in range(5):
        totals = []
        if 0 < step < 4:
            for copy in wide[step]:
                copy.wait()
        for piece in range(16):
            if step < 4:
                split(step, piece)
            if step == 0 and piece % 2 == 1:
                gain[piece // 2] = spread_row(turned, piece // 2)
            if step > 0 and piece in (3, 8, 13):
                totals.append(time_total(step - 1, len(totals)))
        if step > 0:
            j = step - 1
            rows = products(*totals, gain[j], gain[4 + j])
            for part in range(3):
                sums[part * 4 + j : part * 4 + j + 1, :] = rows[part]
    share_sums(sums[...], message, TILE_ROWS)


def update_kernel(start, received, previous, message):
    summed = jnp.sum(received[:, start : start + 8], axis=0)
    updated = 0.5 * (summed[0:1] / (summed[1:2] + 1.0) + previous[...])
    message[...] = jnp.broadcast_to(updated, message.shape)


def iterate_kernel(updated, tile, message, previous, gains_of, sums):
    gains = smoothed(updated, lax.axis_index("sub"))
    gains_of[...] = gains
    previous[...] = gains_of[pl.ds(lax.axis_index("row"), 1), :]
    contract(tile, gains, sums)
    share_sums(sums[...], message, 0)


def last_iterate_kernel(updated, tile, message, gains_of, sums):
    gains = smoothed(updated, lax.axis_index("sub"))
    gains_of[...] = gains
    own = unpack(gains_of[pl.ds(lax.axis_index("row"), 1), :], lax.axis_index("col"))
    contract(tile, gains, sums)
    for peer in range(PEERS):
        message[peer, 0:12] = sums[0:12, :]
        message[peer, 12:20] = own
        message[peer, 20:24] = jnp.zeros((4, 128), F32)


def last_update_kernel(received, mean, rest):
    summed = jnp.sum(received[...], axis=0)
    quotient = summed[0:8] / (twice(summed[8:12]) + 1.0)
    updated = 0.5 * (quotient + summed[12:20])
    means = []
    kept = []
    for part in range(2):
        values = updated[part * 4 : part * 4 + 4]
        total = jnp.sum(values, axis=0, keepdims=True)
        total = (total + swap(total)) / 8.0
        means.append(total)
        kept.append(values - 0.5 * total)
    mean[...] = jnp.broadcast_to(jnp.where(low_lanes(1), means[0], means[1]), (PEERS, 128))
    rest[...] = jnp.concatenate(kept, axis=0)


def share_kernel(means, rest, message):
    overall = jnp.sum(means[...], axis=0, keepdims=True) / 16.0
    other = swap(overall)
    low = low_lanes(1)
    gains = jnp.concatenate(
        [rest[0:4] + jnp.where(low, overall, other), rest[4:8] + jnp.where(low, other, overall)], axis=0
    )
    for peer in range(PEERS):
        message[peer] = gains


def collect_kernel(received, out):
    low = low_lanes(4)
    for part in range(2):
        for pair in range(4):
            even = received[2 * pair, part * 4 : part * 4 + 4]
            odd = received[2 * pair + 1, part * 4 : part * 4 + 4]
            out[part, 0:4, pair * 128 : pair * 128 + 128] = jnp.where(low, even, swap(odd))
            out[part, 4:8, pair * 128 : pair * 128 + 128] = jnp.where(low, swap(even), odd)


def shaped(*shape):
    return jax.ShapeDtypeStruct(shape, F32)


def call(name, kernel, outs, *args, scratch=()):
    return pl.pallas_call(
        kernel,
        out_shape=outs,
        in_specs=[VMEM] * len(args),
        out_specs=jax.tree.map(lambda _: VMEM, outs),
        scratch_shapes=scratch,
        compiler_params=pltpu.CompilerParams(vmem_limit_bytes=4 << 20),
        name=name,
    )(*args)


def exchange(message, axis):
    return lax.all_to_all(message, axis, 0, 0, tiled=True)


def body(visibility, sky_model, antenna_flags, gains_init):
    wide = (2, 2, 4, HALF, HALF * TIMES)
    stay = pl.BlockSpec(memory_space=pl.ANY)
    message, previous = pl.pallas_call(
        first_kernel,
        out_shape=(shaped(PEERS, TILE_ROWS + 8, 128), shaped(1, 128)),
        in_specs=[stay] * 4,
        out_specs=(VMEM, VMEM),
        scratch_shapes=[
            pltpu.VMEM((4, 2, 2, HALF, HALF * TIMES), jnp.bfloat16),
            pltpu.VMEM((4, 2, 2, HALF, HALF * TIMES), jnp.bfloat16),
            pltpu.VMEM((1, 512), jnp.int32),
            pltpu.VMEM((2, 8, 512), F32),
            pltpu.VMEM((2, 6, 128, HALF * TIMES), jnp.bfloat16),
            pltpu.VMEM((8, HALF, 128), F32),
            pltpu.VMEM((16, 128), F32),
            pltpu.SemaphoreType.DMA((2,)),
            pltpu.SemaphoreType.DMA((2, 4)),
        ],
        compiler_params=pltpu.CompilerParams(vmem_limit_bytes=FIRST_LIMIT),
        name="first_kernel",
    )(
        *[
            pltpu.with_memory_space_constraint(value, pltpu.HBM)
            for value in (visibility.reshape(wide), sky_model.reshape(wide), antenna_flags, gains_init)
        ]
    )
    tile = received = exchange(message, "col")
    scratch = [pltpu.VMEM((8, 128), F32), pltpu.VMEM((16, 128), F32)]
    for step in range(2):
        kernel = functools.partial(update_kernel, 0 if step else TILE_ROWS)
        message = call("update_kernel", kernel, shaped(PEERS * PEERS, 128), received, previous)
        updated = exchange(message, ("sub", "row")).reshape(PEERS, PEERS, 128)
        if step == 0:
            outs = (shaped(PEERS, 8, 128), shaped(1, 128))
            message, previous = call("iterate_kernel", iterate_kernel, outs, updated, tile, scratch=scratch)
        else:
            outs = shaped(PEERS, 24, 128)
            message = call("last_iterate_kernel", last_iterate_kernel, outs, updated, tile, scratch=scratch)
        received = exchange(message, "col")
    outs = (shaped(PEERS, 128), shaped(8, 128))
    mean, rest = call("last_update_kernel", last_update_kernel, outs, received)
    means = exchange(mean, "sub")
    message = call("share_kernel", share_kernel, shaped(PEERS, 8, 128), means, rest)
    received = exchange(message, "row")
    return call("collect_kernel", collect_kernel, shaped(2, 8, 512), received)


def solution(mesh):
    return jax.shard_map(
        body,
        mesh=mesh,
        in_specs=(
            P(None, "sub", "row", "col"),
            P(None, "sub", "row", "col"),
            P("sub", None),
            P(None, "sub", None),
        ),
        out_specs=P(None, "sub", None),
        check_vma=False,
    )
```

time: 108 us -> 105 us (0.972)
  Pallas kernels: 7.7 us -> 5.84 us
    pallas_call x7, Pallas kernels: 3.49 us -> 2.01 us  [call(): pl.pallas_call(kernel, out_shape=outs, in_specs=[VMEM] * len(args), out_s...]
where the time goes in v4:
time: 105 us
  blocking collectives  99.1 us (94%)
  Pallas kernels  5.84 us (6%)
    all_to_all x7, blocking collectives, exchange(): return lax.all_to_all(message, axis, 0, 0, tiled=True)  99.1 us
    pallas_call x1, Pallas kernels, body(): pl.pallas_call(first_kernel, out_shape=(shaped(PEERS, TILE_ROWS + 8, 128)...  3.83 us

profile of v4, /device:TPU:1, one launch (start us, length us, event | category | flops | bytes accessed | tf_op | source)
XLA Modules:
  0.0 105.0 jit_solution(16292484751283672308)
XLA Ops:
  0.0 3.8 %first_kernel.1 = (f32[8,104,128]{2,1,0:T(8,128)S(1)}, f32[1,128]{1,0:T(1,128)S(1)}) custom-call(bf16[2,2,4,64,512]{4,3,2,1,0:T(8,128)(2,1)} %bitcast.20, bf16[2,2,4,64,512]{4,3,2,1,0:T(8,128)(2,1)} %bitcast.21, s32[1,512]{1,0:T(1,128)} %flags_hbm.1, f32[2,8,512]{2,1,0:T(8,128)} %init_hbm.1), custom_call_target="tpu_custom_call" | custom-call | tf_op jit(solution)/shard_map/first_kernel/pallas_call | solution.py:317
  3.8 24.5 %all_to_all.49.received.tile = f32[8,104,128]{2,1,0:T(8,128)S(1)} all-to-all(f32[8,104,128]{2,1,0:T(8,128)S(1)} %get-tuple-element.11), channel_id=1, replica_groups=mesh['sub'=8,'row'=8,'col'=8] {'col'}, dimensions={0} | all-to-all | bytes 851968 | tf_op jit(solution)/shard_map/all_to_all | solution.py:311
  28.4 21.8 %all_to_all.50 = f32[64,1,128]{2,1,0:T(1,128)S(1)} all-to-all(f32[64,1,128]{2,1,0:T(1,128)S(1)} %bitcast.16), channel_id=1, replica_groups=mesh['sub'=8,'row'=8,'col'=8] {'sub','row'}, dimensions={0} | all-to-all | bytes 65536 | tf_op jit(solution)/shard_map/all_to_all | solution.py:311
  50.2 0.7 iterate_kernel.1
  50.8 9.3 %all_to_all.51.received = f32[8,8,128]{2,1,0:T(8,128)S(1)} all-to-all(f32[8,8,128]{2,1,0:T(8,128)S(1)} %get-tuple-element.13), channel_id=1, replica_groups=mesh['sub'=8,'row'=8,'col'=8] {'col'}, dimensions={0} | all-to-all | bytes 65536 | tf_op jit(solution)/shard_map/all_to_all | solution.py:311
  60.2 14.5 %all_to_all.52 = f32[64,1,128]{2,1,0:T(1,128)S(1)} all-to-all(f32[64,1,128]{2,1,0:T(1,128)S(1)} %bitcast.17), channel_id=1, replica_groups=mesh['sub'=8,'row'=8,'col'=8] {'sub','row'}, dimensions={0} | all-to-all | bytes 65536 | tf_op jit(solution)/shard_map/all_to_all | solution.py:311
  74.7 0.4 last_iterate_kernel.1
  75.1 9.8 %all_to_all.53.received = f32[8,24,128]{2,1,0:T(8,128)S(1)} all-to-all(f32[8,24,128]{2,1,0:T(8,128)S(1)} %last_iterate_kernel.1), channel_id=1, replica_groups=mesh['sub'=8,'row'=8,'col'=8] {'col'}, dimensions={0} | all-to-all | bytes 196608 | tf_op jit(solution)/shard_map/all_to_all | solution.py:311
  84.9 0.1 last_update_kernel.1
  85.0 8.9 %all_to_all.54 = f32[8,1,128]{2,1,0:T(1,128)S(1)} all-to-all(f32[8,1,128]{2,1,0:T(1,128)S(1)} %bitcast.19), channel_id=1, replica_groups=mesh['sub'=8,'row'=8,'col'=8] {'sub'}, dimensions={0} | all-to-all | bytes 8192 | tf_op jit(solution)/shard_map/all_to_all | solution.py:311
  94.0 0.1 share_kernel.1
  94.0 10.2 %all_to_all.55.received = f32[8,8,128]{2,1,0:T(8,128)S(1)} all-to-all(f32[8,8,128]{2,1,0:T(8,128)S(1)} %share_kernel.1), channel_id=1, replica_groups=mesh['sub'=8,'row'=8,'col'=8] {'row'}, dimensions={0} | all-to-all | bytes 65536 | tf_op jit(solution)/shard_map/all_to_all | solution.py:311
  104.3 0.7 collect_kernel.1
  (2 shorter events, 0.0 us)

commit v5 on v4

--- a/solution.py
+++ b/solution.py
@@ -131,8 +131,8 @@
     numerators = pack_all(summed[0:8])
     denominators = pack_all(twice(summed[8:12]))
     for peer in range(PEERS):
-        rows = [numerators[peer], denominators[peer], jnp.zeros((6, 128), F32)]
-        message[peer, start : start + 8] = jnp.concatenate(rows, axis=0)
+        message[peer, start : start + 1] = numerators[peer]
+        message[peer, start + 1 : start + 2] = denominators[peer]
 
 
 def first_kernel(vis_hbm, sky_hbm, flags_hbm, init_hbm, message, previous, vis, sky, flags, init, parts, gain, sums, small_sems, wide_sems):
@@ -155,7 +155,7 @@
     long = lax.broadcasted_iota(jnp.int32, (HALF, HALF * TIMES), 1)
     short = lax.broadcasted_iota(jnp.int32, (HALF, HALF * TIMES), 0)
     chosen = jnp.where(lax.shift_right_logical(long, 3) == short, 1.0, 0.0).astype(jnp.bfloat16)
-    for copy in small + wide[0]:
+    for copy in small:
         copy.wait()
     low = low_lanes(4)
 
@@ -209,16 +209,16 @@
         return value
 
     turned = wide_gains(col).T
+    for line in range(8):
+        gain[line] = spread_row(turned, line)
     for step in range(5):
         totals = []
-        if 0 < step < 4:
-            for copy in wide[step]:
+        if step < 2:
+            for copy in (wide[0] if step == 0 else sum(wide[1:], [])):
                 copy.wait()
         for piece in range(16):
             if step < 4:
                 split(step, piece)
-            if step == 0 and piece % 2 == 1:
-                gain[piece // 2] = spread_row(turned, piece // 2)
             if step > 0 and piece in (3, 8, 13):
                 totals.append(time_total(step - 1, len(totals)))
         if step > 0:
@@ -230,7 +230,7 @@
 
 
 def update_kernel(start, received, previous, message):
-    summed = jnp.sum(received[:, start : start + 8], axis=0)
+    summed = jnp.sum(received[:, start : start + 2], axis=0)
     updated = 0.5 * (summed[0:1] / (summed[1:2] + 1.0) + previous[...])
     message[...] = jnp.broadcast_to(updated, message.shape)
 
@@ -251,7 +251,6 @@
     for peer in range(PEERS):
         message[peer, 0:12] = sums[0:12, :]
         message[peer, 12:20] = own
-        message[peer, 20:24] = jnp.zeros((4, 128), F32)
 
 
 def last_update_kernel(received, mean, rest):
@@ -316,7 +315,7 @@
     stay = pl.BlockSpec(memory_space=pl.ANY)
     message, previous = pl.pallas_call(
         first_kernel,
-        out_shape=(shaped(PEERS, TILE_ROWS + 8, 128), shaped(1, 128)),
+        out_shape=(shaped(PEERS, TILE_ROWS + 2, 128), shaped(1, 128)),
         in_specs=[stay] * 4,
         out_specs=(VMEM, VMEM),
         scratch_shapes=[
@@ -345,10 +344,10 @@
         message = call("update_kernel", kernel, shaped(PEERS * PEERS, 128), received, previous)
         updated = exchange(message, ("sub", "row")).reshape(PEERS, PEERS, 128)
         if step == 0:
-            outs = (shaped(PEERS, 8, 128), shaped(1, 128))
+            outs = (shaped(PEERS, 2, 128), shaped(1, 128))
             message, previous = call("iterate_kernel", iterate_kernel, outs, updated, tile, scratch=scratch)
         else:
-            outs = shaped(PEERS, 24, 128)
+            outs = shaped(PEERS, 20, 128)
             message = call("last_iterate_kernel", last_iterate_kernel, outs, updated, tile, scratch=scratch)
         received = exchange(message, "col")
     outs = (shaped(PEERS, 128), shaped(8, 128))

time: 105 us -> 105 us (level)
  no operation moved by 1% of the time
where the time goes in v5:
time: 105 us; the launch traced here: 104 us
  blocking collectives  98.8 us (94%)
  Pallas kernels  5.58 us (5%)
    all_to_all x7, blocking collectives, exchange(): return lax.all_to_all(message, axis, 0, 0, tiled=True)  98.8 us
    pallas_call x1, Pallas kernels, body(): pl.pallas_call(first_kernel, out_shape=(shaped(PEERS, TILE_ROWS + 2, 128)...  3.58 us

profile of v5, /device:TPU:1, one launch (start us, length us, event | category | flops | bytes accessed | tf_op | source)
XLA Modules:
  0.0 104.4 jit_solution(7040396416134686183)
XLA Ops:
  0.0 3.6 %first_kernel.1 = (f32[8,98,128]{2,1,0:T(8,128)S(1)}, f32[1,128]{1,0:T(1,128)S(1)}) custom-call(bf16[2,2,4,64,512]{4,3,2,1,0:T(8,128)(2,1)} %bitcast.20, bf16[2,2,4,64,512]{4,3,2,1,0:T(8,128)(2,1)} %bitcast.21, s32[1,512]{1,0:T(1,128)} %flags_hbm.1, f32[2,8,512]{2,1,0:T(8,128)} %init_hbm.1), custom_call_target="tpu_custom_call" | custom-call | tf_op jit(solution)/shard_map/first_kernel/pallas_call | solution.py:316
  3.6 24.6 %all_to_all.49.received.tile = f32[8,98,128]{2,1,0:T(8,128)S(1)} all-to-all(f32[8,98,128]{2,1,0:T(8,128)S(1)} %get-tuple-element.11), channel_id=1, replica_groups=mesh['sub'=8,'row'=8,'col'=8] {'col'}, dimensions={0} | all-to-all | bytes 802816 | tf_op jit(solution)/shard_map/all_to_all | solution.py:310
  28.2 21.8 %all_to_all.50 = f32[64,1,128]{2,1,0:T(1,128)S(1)} all-to-all(f32[64,1,128]{2,1,0:T(1,128)S(1)} %bitcast.16), channel_id=1, replica_groups=mesh['sub'=8,'row'=8,'col'=8] {'sub','row'}, dimensions={0} | all-to-all | bytes 65536 | tf_op jit(solution)/shard_map/all_to_all | solution.py:310
  49.9 0.7 iterate_kernel.1
  50.6 8.9 %all_to_all.51.received = f32[8,2,128]{2,1,0:T(2,128)S(1)} all-to-all(f32[8,2,128]{2,1,0:T(2,128)S(1)} %get-tuple-element.13), channel_id=1, replica_groups=mesh['sub'=8,'row'=8,'col'=8] {'col'}, dimensions={0} | all-to-all | bytes 16384 | tf_op jit(solution)/shard_map/all_to_all | solution.py:310
  59.5 14.6 %all_to_all.52 = f32[64,1,128]{2,1,0:T(1,128)S(1)} all-to-all(f32[64,1,128]{2,1,0:T(1,128)S(1)} %bitcast.17), channel_id=1, replica_groups=mesh['sub'=8,'row'=8,'col'=8] {'sub','row'}, dimensions={0} | all-to-all | bytes 65536 | tf_op jit(solution)/shard_map/all_to_all | solution.py:310
  74.1 0.4 last_iterate_kernel.1
  74.5 9.8 %all_to_all.53.received = f32[8,20,128]{2,1,0:T(8,128)S(1)} all-to-all(f32[8,20,128]{2,1,0:T(8,128)S(1)} %last_iterate_kernel.1), channel_id=1, replica_groups=mesh['sub'=8,'row'=8,'col'=8] {'col'}, dimensions={0} | all-to-all | bytes 163840 | tf_op jit(solution)/shard_map/all_to_all | solution.py:310
  84.4 0.1 last_update_kernel.1
  84.5 8.9 %all_to_all.54 = f32[8,1,128]{2,1,0:T(1,128)S(1)} all-to-all(f32[8,1,128]{2,1,0:T(1,128)S(1)} %bitcast.19), channel_id=1, replica_groups=mesh['sub'=8,'row'=8,'col'=8] {'sub'}, dimensions={0} | all-to-all | bytes 8192 | tf_op jit(solution)/shard_map/all_to_all | solution.py:310
  93.4 0.1 share_kernel.1
  93.5 10.2 %all_to_all.55.received = f32[8,8,128]{2,1,0:T(8,128)S(1)} all-to-all(f32[8,8,128]{2,1,0:T(8,128)S(1)} %share_kernel.1), channel_id=1, replica_groups=mesh['sub'=8,'row'=8,'col'=8] {'row'}, dimensions={0} | all-to-all | bytes 65536 | tf_op jit(solution)/shard_map/all_to_all | solution.py:310
  103.7 0.7 collect_kernel.1
  (2 shorter events, 0.0 us)

commit v6 on v5

--- a/solution.py
+++ b/solution.py
@@ -253,7 +253,7 @@
         message[peer, 12:20] = own
 
 
-def last_update_kernel(received, mean, rest):
+def last_update_kernel(received, message):
     summed = jnp.sum(received[...], axis=0)
     quotient = summed[0:8] / (twice(summed[8:12]) + 1.0)
     updated = 0.5 * (quotient + summed[12:20])
@@ -265,27 +265,31 @@
         total = (total + swap(total)) / 8.0
         means.append(total)
         kept.append(values - 0.5 * total)
-    mean[...] = jnp.broadcast_to(jnp.where(low_lanes(1), means[0], means[1]), (PEERS, 128))
-    rest[...] = jnp.concatenate(kept, axis=0)
-
-
-def share_kernel(means, rest, message):
-    overall = jnp.sum(means[...], axis=0, keepdims=True) / 16.0
+    rest = jnp.concatenate(kept, axis=0)
+    mean = jnp.where(low_lanes(1), means[0], means[1])
+    for peer in range(PEERS):
+        message[peer, 0:8] = rest
+        message[peer, 8:9] = mean
+
+
+def share_kernel(received, message):
+    means = jnp.concatenate([received[block, 8:9] for block in range(PEERS)], axis=0)
+    for peer in range(PEERS):
+        message[peer] = means
+
+
+def collect_kernel(means, received, out):
+    low = low_lanes(4)
+    overall = jnp.sum(means[...], axis=0) / 16.0
     other = swap(overall)
-    low = low_lanes(1)
-    gains = jnp.concatenate(
-        [rest[0:4] + jnp.where(low, overall, other), rest[4:8] + jnp.where(low, other, overall)], axis=0
-    )
-    for peer in range(PEERS):
-        message[peer] = gains
-
-
-def collect_kernel(received, out):
-    low = low_lanes(4)
+    wide = low_lanes(8)
+    added = (jnp.where(wide, overall, other), jnp.where(wide, other, overall))
     for part in range(2):
+        blocks = [
+            received[block, part * 4 : part * 4 + 4] + added[part][block : block + 1] for block in range(PEERS)
+        ]
         for pair in range(4):
-            even = received[2 * pair, part * 4 : part * 4 + 4]
-            odd = received[2 * pair + 1, part * 4 : part * 4 + 4]
+            even, odd = blocks[2 * pair], blocks[2 * pair + 1]
             out[part, 0:4, pair * 128 : pair * 128 + 128] = jnp.where(low, even, swap(odd))
             out[part, 4:8, pair * 128 : pair * 128 + 128] = jnp.where(low, swap(even), odd)
 
@@ -350,12 +354,10 @@
             outs = shaped(PEERS, 20, 128)
             message = call("last_iterate_kernel", last_iterate_kernel, outs, updated, tile, scratch=scratch)
         received = exchange(message, "col")
-    outs = (shaped(PEERS, 128), shaped(8, 128))
-    mean, rest = call("last_update_kernel", last_update_kernel, outs, received)
-    means = exchange(mean, "sub")
-    message = call("share_kernel", share_kernel, shaped(PEERS, 8, 128), means, rest)
+    message = call("last_update_kernel", last_update_kernel, shaped(PEERS, 9, 128), received)
     received = exchange(message, "row")
-    return call("collect_kernel", collect_kernel, shaped(2, 8, 512), received)
+    means = exchange(call("share_kernel", share_kernel, shaped(PEERS, 8, 128), received), "sub")
+    return call("collect_kernel", collect_kernel, shaped(2, 8, 512), means, received)
 
 
 def solution(mesh):

time: 105 us -> 104 us (level)
  no operation moved by 1% of the time
where the time goes in v6:
time: 104 us
  blocking collectives  98.1 us (94%)
  Pallas kernels  5.59 us (5%)
    all_to_all x7, blocking collectives, exchange(): return lax.all_to_all(message, axis, 0, 0, tiled=True)  98.1 us
    pallas_call x1, Pallas kernels, body(): pl.pallas_call(first_kernel, out_shape=(shaped(PEERS, TILE_ROWS + 2, 128)...  3.58 us

profile of v6, /device:TPU:1, one launch (start us, length us, event | category | flops | bytes accessed | tf_op | source)
XLA Modules:
  0.0 103.7 jit_solution(16648413401986885560)
XLA Ops:
  0.0 3.6 %first_kernel.1 = (f32[8,98,128]{2,1,0:T(8,128)S(1)}, f32[1,128]{1,0:T(1,128)S(1)}) custom-call(bf16[2,2,4,64,512]{4,3,2,1,0:T(8,128)(2,1)} %bitcast.14, bf16[2,2,4,64,512]{4,3,2,1,0:T(8,128)(2,1)} %bitcast.15, s32[1,512]{1,0:T(1,128)} %flags_hbm.1, f32[2,8,512]{2,1,0:T(8,128)} %init_hbm.1), custom_call_target="tpu_custom_call" | custom-call | tf_op jit(solution)/shard_map/first_kernel/pallas_call | solution.py:320
  3.6 24.6 %all_to_all.43.received.tile = f32[8,98,128]{2,1,0:T(8,128)S(1)} all-to-all(f32[8,98,128]{2,1,0:T(8,128)S(1)} %get-tuple-element.9), channel_id=1, replica_groups=mesh['sub'=8,'row'=8,'col'=8] {'col'}, dimensions={0} | all-to-all | bytes 802816 | tf_op jit(solution)/shard_map/all_to_all | solution.py:314
  28.2 21.8 %all_to_all.44 = f32[64,1,128]{2,1,0:T(1,128)S(1)} all-to-all(f32[64,1,128]{2,1,0:T(1,128)S(1)} %bitcast.12), channel_id=1, replica_groups=mesh['sub'=8,'row'=8,'col'=8] {'sub','row'}, dimensions={0} | all-to-all | bytes 65536 | tf_op jit(solution)/shard_map/all_to_all | solution.py:314
  49.9 0.7 iterate_kernel.1
  50.6 8.9 %all_to_all.45.received = f32[8,2,128]{2,1,0:T(2,128)S(1)} all-to-all(f32[8,2,128]{2,1,0:T(2,128)S(1)} %get-tuple-element.11), channel_id=1, replica_groups=mesh['sub'=8,'row'=8,'col'=8] {'col'}, dimensions={0} | all-to-all | bytes 16384 | tf_op jit(solution)/shard_map/all_to_all | solution.py:314
  59.5 14.6 %all_to_all.46 = f32[64,1,128]{2,1,0:T(1,128)S(1)} all-to-all(f32[64,1,128]{2,1,0:T(1,128)S(1)} %bitcast.13), channel_id=1, replica_groups=mesh['sub'=8,'row'=8,'col'=8] {'sub','row'}, dimensions={0} | all-to-all | bytes 65536 | tf_op jit(solution)/shard_map/all_to_all | solution.py:314
  74.1 0.4 last_iterate_kernel.1
  74.5 9.8 %all_to_all.47.received = f32[8,20,128]{2,1,0:T(8,128)S(1)} all-to-all(f32[8,20,128]{2,1,0:T(8,128)S(1)} %last_iterate_kernel.1), channel_id=1, replica_groups=mesh['sub'=8,'row'=8,'col'=8] {'col'}, dimensions={0} | all-to-all | bytes 163840 | tf_op jit(solution)/shard_map/all_to_all | solution.py:314
  84.4 0.1 last_update_kernel.1
  84.5 9.2 %all_to_all.48.received = f32[8,9,128]{2,1,0:T(8,128)S(1)} all-to-all(f32[8,9,128]{2,1,0:T(8,128)S(1)} %last_update_kernel.1), channel_id=1, replica_groups=mesh['sub'=8,'row'=8,'col'=8] {'row'}, dimensions={0} | all-to-all | bytes 73728 | tf_op jit(solution)/shard_map/all_to_all | solution.py:314
  93.7 9.2 %all_to_all.49.means = f32[8,8,128]{2,1,0:T(8,128)S(1)} all-to-all(f32[8,8,128]{2,1,0:T(8,128)S(1)} %share_kernel.1), channel_id=1, replica_groups=mesh['sub'=8,'row'=8,'col'=8] {'sub'}, dimensions={0} | all-to-all | bytes 65536 | tf_op jit(solution)/shard_map/all_to_all | solution.py:314
  102.9 0.8 collect_kernel.1
  (3 shorter events, 0.0 us)

commit v7 on v6

--- a/solution.py
+++ b/solution.py
@@ -29,10 +29,14 @@
     return jnp.where(odd, swap(slab), slab)
 
 
-def spread_row(turned, row):
-    first = jnp.broadcast_to(turned[:HALF, row : row + 1], (HALF, 128))
-    second = jnp.broadcast_to(turned[HALF:, row : row + 1], (HALF, 128))
-    return jnp.where(low_lanes(HALF), first, second)
+def beside(gains):
+    turned = jnp.concatenate([gains, swap(gains)], axis=0).T
+    return jnp.concatenate([turned[:HALF], jnp.zeros((HALF, 112), F32)], axis=1)
+
+
+def pick(columns, which):
+    at = jnp.where(low_lanes(columns.shape[0]), which, which + 8)
+    return jnp.take_along_axis(columns, at, axis=1)
 
 
 def products(cross_re, cross_im, power, gain_re, gain_im):
@@ -56,35 +60,26 @@
     return out
 
 
+def group_of(rows):
+    return lax.shift_right_logical(lanes_of(rows) & (HALF - 1), 3)
+
+
 def pack_all(wide):
-    lane = lanes_of(8)
-    own = lax.shift_right_logical(lane, 4) == lax.broadcasted_iota(jnp.int32, (8, 128), 0)
-    near = own & ((lane & 8) == 0)
-    far = own & ((lane & 8) != 0)
-    moved = slide(wide, 16)
+    own = group_of(8) == lax.broadcasted_iota(jnp.int32, (8, 128), 0)
+    moved = slide(wide, 8)
     rows = []
     for which in range(8):
-        first = pltpu.roll(moved, (128 - 8 * which) % 128, 1)
-        second = pltpu.roll(moved, (200 - 8 * which) % 128, 1)
-        value = jnp.where(near, first, jnp.where(far, second, 0.0))
+        value = jnp.where(own, pltpu.roll(moved, (128 - 8 * which) % 128, 1), 0.0)
         rows.append(jnp.sum(value, axis=0, keepdims=True))
     return rows
 
 
-def unpack(packed, which):
-    group = lax.shift_right_logical(lanes_of(8), 3)
-    moved = slide(jnp.broadcast_to(packed, (8, 128)), 112)
-    first = pltpu.roll(moved, 8 * which, 1)
-    second = pltpu.roll(moved, (8 * which + 56) % 128, 1)
-    return jnp.where(group == which, first, jnp.where(group == which + 8, second, 0.0))
-
-
 def channel_mean(packed):
-    lane = lanes_of(8) & (HALF - 1)
+    lane = lanes_of(8) & 31
     total = packed
-    for step in range(8, HALF, 8):
-        total = total + jnp.where(lane >= step, pltpu.roll(packed, step, 1), pltpu.roll(packed, step + HALF, 1))
-    return total / 8.0
+    for step in (8, 16, 24):
+        total = total + jnp.where(lane >= step, pltpu.roll(packed, step, 1), pltpu.roll(packed, step + 96, 1))
+    return (total + swap(total)) / 8.0
 
 
 def smoothed(updated, sub):
@@ -93,34 +88,22 @@
     return own + 0.5 * channel_mean(overall - own)
 
 
-def spread_packed(gains):
-    turned = gains.T
-    low = low_lanes(8)
-    columns = []
-    for row in range(8):
-        pieces = []
-        for which in range(8):
-            first = jnp.broadcast_to(turned[row * 16 : row * 16 + 8, which : which + 1], (8, 128))
-            second = jnp.broadcast_to(turned[row * 16 + 8 : row * 16 + 16, which : which + 1], (8, 128))
-            pieces.append(jnp.where(low, first, second))
-        columns.append(pieces)
-    return columns[:4], columns[4:]
-
-
 def contract(tile, gains, sums):
-    gain_re, gain_im = spread_packed(gains)
-    for j in range(4):
-        totals = [jnp.zeros((8, 128), F32)] * 3
-        for which in range(8):
+    turned = beside(gains)
+    columns = [turned[row * 8 : row * 8 + 8] for row in range(8)]
+    totals = [[None] * 3 for _ in range(4)]
+    for which in range(8):
+        gain = [pick(column, which) for column in columns]
+        for j in range(4):
             cross_re, cross_im, power = [
                 tile[which, (part * 4 + j) * 8 : (part * 4 + j) * 8 + 8] for part in range(3)
             ]
-            re, im = gain_re[j][which], gain_im[j][which]
-            totals[0] += cross_re * re - cross_im * im
-            totals[1] += cross_re * im + cross_im * re
-            totals[2] += power * (re * re + im * im)
+            re, im = gain[j], gain[4 + j]
+            terms = (cross_re * re - cross_im * im, cross_re * im + cross_im * re, power * (re * re + im * im))
+            totals[j] = [term if which == 0 else total + term for total, term in zip(totals[j], terms)]
+    for j in range(4):
         for part in range(3):
-            sums[part * 4 + j : part * 4 + j + 1, :] = jnp.sum(totals[part], axis=0, keepdims=True)
+            sums[part * 4 + j : part * 4 + j + 1, :] = jnp.sum(totals[j][part], axis=0, keepdims=True)
 
 
 def twice(rows):
@@ -208,9 +191,9 @@
             message[peer, at : at + 8] = value[peer * 8 : peer * 8 + 8]
         return value
 
-    turned = wide_gains(col).T
+    columns = beside(wide_gains(col))
     for line in range(8):
-        gain[line] = spread_row(turned, line)
+        gain[line] = pick(columns, line)
     for step in range(5):
         totals = []
         if step < 2:
@@ -246,17 +229,18 @@
 def last_iterate_kernel(updated, tile, message, gains_of, sums):
     gains = smoothed(updated, lax.axis_index("sub"))
     gains_of[...] = gains
-    own = unpack(gains_of[pl.ds(lax.axis_index("row"), 1), :], lax.axis_index("col"))
+    own = gains_of[pl.ds(lax.axis_index("row"), 1), :]
     contract(tile, gains, sums)
     for peer in range(PEERS):
         message[peer, 0:12] = sums[0:12, :]
-        message[peer, 12:20] = own
+        message[peer, 12:13] = own
 
 
 def last_update_kernel(received, message):
-    summed = jnp.sum(received[...], axis=0)
+    summed = jnp.sum(received[:, 0:12], axis=0)
+    previous = jnp.concatenate([received[peer, 12:13] for peer in range(PEERS)], axis=0)
     quotient = summed[0:8] / (twice(summed[8:12]) + 1.0)
-    updated = 0.5 * (quotient + summed[12:20])
+    updated = 0.5 * (quotient + jnp.concatenate(pack_all(previous), axis=0))
     means = []
     kept = []
     for part in range(2):
@@ -351,7 +335,7 @@
             outs = (shaped(PEERS, 2, 128), shaped(1, 128))
             message, previous = call("iterate_kernel", iterate_kernel, outs, updated, tile, scratch=scratch)
         else:
-            outs = shaped(PEERS, 20, 128)
+            outs = shaped(PEERS, 13, 128)
             message = call("last_iterate_kernel", last_iterate_kernel, outs, updated, tile, scratch=scratch)
         received = exchange(message, "col")
     message = call("last_update_kernel", last_update_kernel, shaped(PEERS, 9, 128), received)

time: 104 us -> 104 us (level)
  no operation moved by 1% of the time
where the time goes in v7:
time: 104 us
  blocking collectives  97.7 us (94%)
  Pallas kernels  5.96 us (6%)
    all_to_all x7, blocking collectives, exchange(): return lax.all_to_all(message, axis, 0, 0, tiled=True)  97.7 us
    pallas_call x1, Pallas kernels, body(): pl.pallas_call(first_kernel, out_shape=(shaped(PEERS, TILE_ROWS + 2, 128)...  3.61 us
    pallas_call x7, Pallas kernels, call(): pl.pallas_call(kernel, out_shape=outs, in_specs=[VMEM] * len(args), out_s...  2.36 us

profile of v7, /device:TPU:1, one launch (start us, length us, event | category | flops | bytes accessed | tf_op | source)
XLA Modules:
  0.0 103.7 jit_solution(2702651670191589925)
XLA Ops:
  0.0 3.6 %first_kernel.1 = (f32[8,98,128]{2,1,0:T(8,128)S(1)}, f32[1,128]{1,0:T(1,128)S(1)}) custom-call(bf16[2,2,4,64,512]{4,3,2,1,0:T(8,128)(2,1)} %bitcast.14, bf16[2,2,4,64,512]{4,3,2,1,0:T(8,128)(2,1)} %bitcast.15, s32[1,512]{1,0:T(1,128)} %flags_hbm.1, f32[2,8,512]{2,1,0:T(8,128)} %init_hbm.1), custom_call_target="tpu_custom_call" | custom-call | tf_op jit(solution)/shard_map/first_kernel/pallas_call | solution.py:304
  3.6 24.5 %all_to_all.43.received.tile = f32[8,98,128]{2,1,0:T(8,128)S(1)} all-to-all(f32[8,98,128]{2,1,0:T(8,128)S(1)} %get-tuple-element.9), channel_id=1, replica_groups=mesh['sub'=8,'row'=8,'col'=8] {'col'}, dimensions={0} | all-to-all | bytes 802816 | tf_op jit(solution)/shard_map/all_to_all | solution.py:298
  28.2 21.8 %all_to_all.44 = f32[64,1,128]{2,1,0:T(1,128)S(1)} all-to-all(f32[64,1,128]{2,1,0:T(1,128)S(1)} %bitcast.12), channel_id=1, replica_groups=mesh['sub'=8,'row'=8,'col'=8] {'sub','row'}, dimensions={0} | all-to-all | bytes 65536 | tf_op jit(solution)/shard_map/all_to_all | solution.py:298
  49.9 0.7 iterate_kernel.1
  50.7 8.9 %all_to_all.45.received = f32[8,2,128]{2,1,0:T(2,128)S(1)} all-to-all(f32[8,2,128]{2,1,0:T(2,128)S(1)} %get-tuple-element.11), channel_id=1, replica_groups=mesh['sub'=8,'row'=8,'col'=8] {'col'}, dimensions={0} | all-to-all | bytes 16384 | tf_op jit(solution)/shard_map/all_to_all | solution.py:298
  59.6 14.6 %all_to_all.46 = f32[64,1,128]{2,1,0:T(1,128)S(1)} all-to-all(f32[64,1,128]{2,1,0:T(1,128)S(1)} %bitcast.13), channel_id=1, replica_groups=mesh['sub'=8,'row'=8,'col'=8] {'sub','row'}, dimensions={0} | all-to-all | bytes 65536 | tf_op jit(solution)/shard_map/all_to_all | solution.py:298
  74.2 0.6 last_iterate_kernel.1
  74.8 9.6 %all_to_all.47.received = f32[8,13,128]{2,1,0:T(8,128)S(1)} all-to-all(f32[8,13,128]{2,1,0:T(8,128)S(1)} %last_iterate_kernel.1), channel_id=1, replica_groups=mesh['sub'=8,'row'=8,'col'=8] {'col'}, dimensions={0} | all-to-all | bytes 106496 | tf_op jit(solution)/shard_map/all_to_all | solution.py:298
  84.4 0.2 last_update_kernel.1
  84.6 9.0 %all_to_all.48.received = f32[8,9,128]{2,1,0:T(8,128)S(1)} all-to-all(f32[8,9,128]{2,1,0:T(8,128)S(1)} %last_update_kernel.1), channel_id=1, replica_groups=mesh['sub'=8,'row'=8,'col'=8] {'row'}, dimensions={0} | all-to-all | bytes 73728 | tf_op jit(solution)/shard_map/all_to_all | solution.py:298
  93.7 9.2 %all_to_all.49.means = f32[8,8,128]{2,1,0:T(8,128)S(1)} all-to-all(f32[8,8,128]{2,1,0:T(8,128)S(1)} %share_kernel.1), channel_id=1, replica_groups=mesh['sub'=8,'row'=8,'col'=8] {'sub'}, dimensions={0} | all-to-all | bytes 65536 | tf_op jit(solution)/shard_map/all_to_all | solution.py:298
  102.9 0.8 collect_kernel.1
  (3 shorter events, 0.0 us)

commit v8 on v7

--- a/solution.py
+++ b/solution.py
@@ -29,14 +29,10 @@
     return jnp.where(odd, swap(slab), slab)
 
 
-def beside(gains):
-    turned = jnp.concatenate([gains, swap(gains)], axis=0).T
-    return jnp.concatenate([turned[:HALF], jnp.zeros((HALF, 112), F32)], axis=1)
-
-
-def pick(columns, which):
-    at = jnp.where(low_lanes(columns.shape[0]), which, which + 8)
-    return jnp.take_along_axis(columns, at, axis=1)
+def pick(turned, low, row, size, which):
+    first = jnp.broadcast_to(turned[row : row + size, which : which + 1], (size, 128))
+    second = jnp.broadcast_to(turned[row + HALF : row + HALF + size, which : which + 1], (size, 128))
+    return jnp.where(low, first, second)
 
 
 def products(cross_re, cross_im, power, gain_re, gain_im):
@@ -89,11 +85,11 @@
 
 
 def contract(tile, gains, sums):
-    turned = beside(gains)
-    columns = [turned[row * 8 : row * 8 + 8] for row in range(8)]
+    turned = gains.T
+    low = low_lanes(8)
     totals = [[None] * 3 for _ in range(4)]
     for which in range(8):
-        gain = [pick(column, which) for column in columns]
+        gain = [pick(turned, low, row * 8, 8, which) for row in range(8)]
         for j in range(4):
             cross_re, cross_im, power = [
                 tile[which, (part * 4 + j) * 8 : (part * 4 + j) * 8 + 8] for part in range(3)
@@ -191,9 +187,9 @@
             message[peer, at : at + 8] = value[peer * 8 : peer * 8 + 8]
         return value
 
-    columns = beside(wide_gains(col))
+    turned = wide_gains(col).T
     for line in range(8):
-        gain[line] = pick(columns, line)
+        gain[line] = pick(turned, low_lanes(HALF), 0, HALF, line)
     for step in range(5):
         totals = []
         if step < 2:

time: 104 us -> 104 us (level)
  no operation moved by 1% of the time
where the time goes in v8:
time: 104 us
  blocking collectives  97.7 us (94%)
  Pallas kernels  5.83 us (6%)
    all_to_all x7, blocking collectives, exchange(): return lax.all_to_all(message, axis, 0, 0, tiled=True)  97.7 us
    pallas_call x1, Pallas kernels, body(): pl.pallas_call(first_kernel, out_shape=(shaped(PEERS, TILE_ROWS + 2, 128)...  3.59 us
    pallas_call x7, Pallas kernels, call(): pl.pallas_call(kernel, out_shape=outs, in_specs=[VMEM] * len(args), out_s...  2.24 us

profile of v8, /device:TPU:1, one launch (start us, length us, event | category | flops | bytes accessed | tf_op | source)
XLA Modules:
  0.0 103.6 jit_solution(5167786462201012559)
XLA Ops:
  0.0 3.6 %first_kernel.1 = (f32[8,98,128]{2,1,0:T(8,128)S(1)}, f32[1,128]{1,0:T(1,128)S(1)}) custom-call(bf16[2,2,4,64,512]{4,3,2,1,0:T(8,128)(2,1)} %bitcast.14, bf16[2,2,4,64,512]{4,3,2,1,0:T(8,128)(2,1)} %bitcast.15, s32[1,512]{1,0:T(1,128)} %flags_hbm.1, f32[2,8,512]{2,1,0:T(8,128)} %init_hbm.1), custom_call_target="tpu_custom_call" | custom-call | tf_op jit(solution)/shard_map/first_kernel/pallas_call | solution.py:300
  3.6 24.5 %all_to_all.43.received.tile = f32[8,98,128]{2,1,0:T(8,128)S(1)} all-to-all(f32[8,98,128]{2,1,0:T(8,128)S(1)} %get-tuple-element.9), channel_id=1, replica_groups=mesh['sub'=8,'row'=8,'col'=8] {'col'}, dimensions={0} | all-to-all | bytes 802816 | tf_op jit(solution)/shard_map/all_to_all | solution.py:294
  28.2 21.8 %all_to_all.44 = f32[64,1,128]{2,1,0:T(1,128)S(1)} all-to-all(f32[64,1,128]{2,1,0:T(1,128)S(1)} %bitcast.12), channel_id=1, replica_groups=mesh['sub'=8,'row'=8,'col'=8] {'sub','row'}, dimensions={0} | all-to-all | bytes 65536 | tf_op jit(solution)/shard_map/all_to_all | solution.py:294
  49.9 0.7 iterate_kernel.1
  50.6 8.9 %all_to_all.45.received = f32[8,2,128]{2,1,0:T(2,128)S(1)} all-to-all(f32[8,2,128]{2,1,0:T(2,128)S(1)} %get-tuple-element.11), channel_id=1, replica_groups=mesh['sub'=8,'row'=8,'col'=8] {'col'}, dimensions={0} | all-to-all | bytes 16384 | tf_op jit(solution)/shard_map/all_to_all | solution.py:294
  59.6 14.6 %all_to_all.46 = f32[64,1,128]{2,1,0:T(1,128)S(1)} all-to-all(f32[64,1,128]{2,1,0:T(1,128)S(1)} %bitcast.13), channel_id=1, replica_groups=mesh['sub'=8,'row'=8,'col'=8] {'sub','row'}, dimensions={0} | all-to-all | bytes 65536 | tf_op jit(solution)/shard_map/all_to_all | solution.py:294
  74.1 0.5 last_iterate_kernel.1
  74.7 9.6 %all_to_all.47.received = f32[8,13,128]{2,1,0:T(8,128)S(1)} all-to-all(f32[8,13,128]{2,1,0:T(8,128)S(1)} %last_iterate_kernel.1), channel_id=1, replica_groups=mesh['sub'=8,'row'=8,'col'=8] {'col'}, dimensions={0} | all-to-all | bytes 106496 | tf_op jit(solution)/shard_map/all_to_all | solution.py:294
  84.3 0.2 last_update_kernel.1
  84.5 9.0 %all_to_all.48.received = f32[8,9,128]{2,1,0:T(8,128)S(1)} all-to-all(f32[8,9,128]{2,1,0:T(8,128)S(1)} %last_update_kernel.1), channel_id=1, replica_groups=mesh['sub'=8,'row'=8,'col'=8] {'row'}, dimensions={0} | all-to-all | bytes 73728 | tf_op jit(solution)/shard_map/all_to_all | solution.py:294
  93.5 9.2 %all_to_all.49.means = f32[8,8,128]{2,1,0:T(8,128)S(1)} all-to-all(f32[8,8,128]{2,1,0:T(8,128)S(1)} %share_kernel.1), channel_id=1, replica_groups=mesh['sub'=8,'row'=8,'col'=8] {'sub'}, dimensions={0} | all-to-all | bytes 65536 | tf_op jit(solution)/shard_map/all_to_all | solution.py:294
  102.8 0.8 collect_kernel.1
  (3 shorter events, 0.0 us)

commit v9 on v8

--- a/solution.py
+++ b/solution.py
@@ -87,19 +87,19 @@
 def contract(tile, gains, sums):
     turned = gains.T
     low = low_lanes(8)
-    totals = [[None] * 3 for _ in range(4)]
-    for which in range(8):
-        gain = [pick(turned, low, row * 8, 8, which) for row in range(8)]
-        for j in range(4):
+    gain = [[pick(turned, low, row * 8, 8, which) for which in range(8)] for row in range(8)]
+    for j in range(4):
+        totals = [jnp.zeros((8, 128), F32)] * 3
+        for which in range(8):
             cross_re, cross_im, power = [
                 tile[which, (part * 4 + j) * 8 : (part * 4 + j) * 8 + 8] for part in range(3)
             ]
-            re, im = gain[j], gain[4 + j]
-            terms = (cross_re * re - cross_im * im, cross_re * im + cross_im * re, power * (re * re + im * im))
-            totals[j] = [term if which == 0 else total + term for total, term in zip(totals[j], terms)]
-    for j in range(4):
+            re, im = gain[j][which], gain[4 + j][which]
+            totals[0] += cross_re * re - cross_im * im
+            totals[1] += cross_re * im + cross_im * re
+            totals[2] += power * (re * re + im * im)
         for part in range(3):
-            sums[part * 4 + j : part * 4 + j + 1, :] = jnp.sum(totals[j][part], axis=0, keepdims=True)
+            sums[part * 4 + j : part * 4 + j + 1, :] = jnp.sum(totals[part], axis=0, keepdims=True)
 
 
 def twice(rows):

time: 104 us -> 104 us (level)
  no operation moved by 1% of the time
where the time goes in v9:
time: 104 us
  blocking collectives  97.7 us (94%)
  Pallas kernels  5.82 us (6%)
    all_to_all x7, blocking collectives, exchange(): return lax.all_to_all(message, axis, 0, 0, tiled=True)  97.7 us
    pallas_call x1, Pallas kernels, body(): pl.pallas_call(first_kernel, out_shape=(shaped(PEERS, TILE_ROWS + 2, 128)...  3.59 us
    pallas_call x7, Pallas kernels, call(): pl.pallas_call(kernel, out_shape=outs, in_specs=[VMEM] * len(args), out_s...  2.23 us

profile of v9, /device:TPU:1, one launch (start us, length us, event | category | flops | bytes accessed | tf_op | source)
XLA Modules:
  0.0 103.6 jit_solution(12474170102671122792)
XLA Ops:
  0.0 3.6 %first_kernel.1 = (f32[8,98,128]{2,1,0:T(8,128)S(1)}, f32[1,128]{1,0:T(1,128)S(1)}) custom-call(bf16[2,2,4,64,512]{4,3,2,1,0:T(8,128)(2,1)} %bitcast.14, bf16[2,2,4,64,512]{4,3,2,1,0:T(8,128)(2,1)} %bitcast.15, s32[1,512]{1,0:T(1,128)} %flags_hbm.1, f32[2,8,512]{2,1,0:T(8,128)} %init_hbm.1), custom_call_target="tpu_custom_call" | custom-call | tf_op jit(solution)/shard_map/first_kernel/pallas_call | solution.py:300
  3.6 24.5 %all_to_all.43.received.tile = f32[8,98,128]{2,1,0:T(8,128)S(1)} all-to-all(f32[8,98,128]{2,1,0:T(8,128)S(1)} %get-tuple-element.9), channel_id=1, replica_groups=mesh['sub'=8,'row'=8,'col'=8] {'col'}, dimensions={0} | all-to-all | bytes 802816 | tf_op jit(solution)/shard_map/all_to_all | solution.py:294
  28.2 21.8 %all_to_all.44 = f32[64,1,128]{2,1,0:T(1,128)S(1)} all-to-all(f32[64,1,128]{2,1,0:T(1,128)S(1)} %bitcast.12), channel_id=1, replica_groups=mesh['sub'=8,'row'=8,'col'=8] {'sub','row'}, dimensions={0} | all-to-all | bytes 65536 | tf_op jit(solution)/shard_map/all_to_all | solution.py:294
  49.9 0.7 iterate_kernel.1
  50.6 8.9 %all_to_all.45.received = f32[8,2,128]{2,1,0:T(2,128)S(1)} all-to-all(f32[8,2,128]{2,1,0:T(2,128)S(1)} %get-tuple-element.11), channel_id=1, replica_groups=mesh['sub'=8,'row'=8,'col'=8] {'col'}, dimensions={0} | all-to-all | bytes 16384 | tf_op jit(solution)/shard_map/all_to_all | solution.py:294
  59.6 14.6 %all_to_all.46 = f32[64,1,128]{2,1,0:T(1,128)S(1)} all-to-all(f32[64,1,128]{2,1,0:T(1,128)S(1)} %bitcast.13), channel_id=1, replica_groups=mesh['sub'=8,'row'=8,'col'=8] {'sub','row'}, dimensions={0} | all-to-all | bytes 65536 | tf_op jit(solution)/shard_map/all_to_all | solution.py:294
  74.1 0.5 last_iterate_kernel.1
  74.6 9.6 %all_to_all.47.received = f32[8,13,128]{2,1,0:T(8,128)S(1)} all-to-all(f32[8,13,128]{2,1,0:T(8,128)S(1)} %last_iterate_kernel.1), channel_id=1, replica_groups=mesh['sub'=8,'row'=8,'col'=8] {'col'}, dimensions={0} | all-to-all | bytes 106496 | tf_op jit(solution)/shard_map/all_to_all | solution.py:294
  84.2 0.2 last_update_kernel.1
  84.5 9.0 %all_to_all.48.received = f32[8,9,128]{2,1,0:T(8,128)S(1)} all-to-all(f32[8,9,128]{2,1,0:T(8,128)S(1)} %last_update_kernel.1), channel_id=1, replica_groups=mesh['sub'=8,'row'=8,'col'=8] {'row'}, dimensions={0} | all-to-all | bytes 73728 | tf_op jit(solution)/shard_map/all_to_all | solution.py:294
  93.5 9.2 %all_to_all.49.means = f32[8,8,128]{2,1,0:T(8,128)S(1)} all-to-all(f32[8,8,128]{2,1,0:T(8,128)S(1)} %share_kernel.1), channel_id=1, replica_groups=mesh['sub'=8,'row'=8,'col'=8] {'sub'}, dimensions={0} | all-to-all | bytes 65536 | tf_op jit(solution)/shard_map/all_to_all | solution.py:294
  102.8 0.8 collect_kernel.1
  (3 shorter events, 0.0 us)

commit v10 on v8

--- a/solution.py
+++ b/solution.py
@@ -192,8 +192,8 @@
         gain[line] = pick(turned, low_lanes(HALF), 0, HALF, line)
     for step in range(5):
         totals = []
-        if step < 2:
-            for copy in (wide[0] if step == 0 else sum(wide[1:], [])):
+        if step == 0:
+            for copy in sum(wide, []):
                 copy.wait()
         for piece in range(16):
             if step < 4:

time: 104 us -> 104 us (level)
  no operation moved by 1% of the time
where the time goes in v10:
time: 104 us; the launch traced here: 103 us
  blocking collectives  97.7 us (94%)
  Pallas kernels  5.74 us (6%)
    all_to_all x7, blocking collectives, exchange(): return lax.all_to_all(message, axis, 0, 0, tiled=True)  97.7 us
    pallas_call x1, Pallas kernels, body(): pl.pallas_call(first_kernel, out_shape=(shaped(PEERS, TILE_ROWS + 2, 128)...  3.5 us
    pallas_call x7, Pallas kernels, call(): pl.pallas_call(kernel, out_shape=outs, in_specs=[VMEM] * len(args), out_s...  2.24 us

profile of v10, /device:TPU:1, one launch (start us, length us, event | category | flops | bytes accessed | tf_op | source)
XLA Modules:
  0.0 103.5 jit_solution(2007525798467782655)
XLA Ops:
  0.0 3.5 %first_kernel.1 = (f32[8,98,128]{2,1,0:T(8,128)S(1)}, f32[1,128]{1,0:T(1,128)S(1)}) custom-call(bf16[2,2,4,64,512]{4,3,2,1,0:T(8,128)(2,1)} %bitcast.14, bf16[2,2,4,64,512]{4,3,2,1,0:T(8,128)(2,1)} %bitcast.15, s32[1,512]{1,0:T(1,128)} %flags_hbm.1, f32[2,8,512]{2,1,0:T(8,128)} %init_hbm.1), custom_call_target="tpu_custom_call" | custom-call | tf_op jit(solution)/shard_map/first_kernel/pallas_call | solution.py:300
  3.5 24.6 %all_to_all.43.received.tile = f32[8,98,128]{2,1,0:T(8,128)S(1)} all-to-all(f32[8,98,128]{2,1,0:T(8,128)S(1)} %get-tuple-element.9), channel_id=1, replica_groups=mesh['sub'=8,'row'=8,'col'=8] {'col'}, dimensions={0} | all-to-all | bytes 802816 | tf_op jit(solution)/shard_map/all_to_all | solution.py:294
  28.1 21.8 %all_to_all.44 = f32[64,1,128]{2,1,0:T(1,128)S(1)} all-to-all(f32[64,1,128]{2,1,0:T(1,128)S(1)} %bitcast.12), channel_id=1, replica_groups=mesh['sub'=8,'row'=8,'col'=8] {'sub','row'}, dimensions={0} | all-to-all | bytes 65536 | tf_op jit(solution)/shard_map/all_to_all | solution.py:294
  49.8 0.7 iterate_kernel.1
  50.5 8.9 %all_to_all.45.received = f32[8,2,128]{2,1,0:T(2,128)S(1)} all-to-all(f32[8,2,128]{2,1,0:T(2,128)S(1)} %get-tuple-element.11), channel_id=1, replica_groups=mesh['sub'=8,'row'=8,'col'=8] {'col'}, dimensions={0} | all-to-all | bytes 16384 | tf_op jit(solution)/shard_map/all_to_all | solution.py:294
  59.5 14.6 %all_to_all.46 = f32[64,1,128]{2,1,0:T(1,128)S(1)} all-to-all(f32[64,1,128]{2,1,0:T(1,128)S(1)} %bitcast.13), channel_id=1, replica_groups=mesh['sub'=8,'row'=8,'col'=8] {'sub','row'}, dimensions={0} | all-to-all | bytes 65536 | tf_op jit(solution)/shard_map/all_to_all | solution.py:294
  74.0 0.5 last_iterate_kernel.1
  74.6 9.6 %all_to_all.47.received = f32[8,13,128]{2,1,0:T(8,128)S(1)} all-to-all(f32[8,13,128]{2,1,0:T(8,128)S(1)} %last_iterate_kernel.1), channel_id=1, replica_groups=mesh['sub'=8,'row'=8,'col'=8] {'col'}, dimensions={0} | all-to-all | bytes 106496 | tf_op jit(solution)/shard_map/all_to_all | solution.py:294
  84.2 0.2 last_update_kernel.1
  84.4 9.0 %all_to_all.48.received = f32[8,9,128]{2,1,0:T(8,128)S(1)} all-to-all(f32[8,9,128]{2,1,0:T(8,128)S(1)} %last_update_kernel.1), channel_id=1, replica_groups=mesh['sub'=8,'row'=8,'col'=8] {'row'}, dimensions={0} | all-to-all | bytes 73728 | tf_op jit(solution)/shard_map/all_to_all | solution.py:294
  93.4 9.2 %all_to_all.49.means = f32[8,8,128]{2,1,0:T(8,128)S(1)} all-to-all(f32[8,8,128]{2,1,0:T(8,128)S(1)} %share_kernel.1), channel_id=1, replica_groups=mesh['sub'=8,'row'=8,'col'=8] {'sub'}, dimensions={0} | all-to-all | bytes 65536 | tf_op jit(solution)/shard_map/all_to_all | solution.py:294
  102.7 0.8 collect_kernel.1
  (3 shorter events, 0.0 us)
